TPU v7x, 32 devices: a whole 2x2x4 slice. The times are simulated.
32 devices in a mesh: phase: 2 (over x), slab: 8 (over z, y), arm: 2 (over core).
Axes of the slice: x: 2, y: 2, z: 4, core: 2. Of those that a mesh axis runs over, the one named last changes fastest.
Arguments:
- field_w: float32 [2, 64, 32, 128], P(None, ('phase', 'slab')), parts along dimension 1, may hold values from -0.6 to 0.6, as said below
- metric: float32 [12], P('phase'), parts along dimension 0, may hold values from -0.25 to 1, as said below
- arm_length: float32 [16], P('arm'), may hold values from 0.4 to 1
- arm_steps: int32 [16], P('arm'), may hold values from 8 to 16
- arm_species: int32 [16], P('arm'), may hold values from 0 to 1
Outputs:
- density: float32 [2, 64, 32, 128], P(None, ('phase', 'slab'), 'arm'), parts along dimension 1
- stress: float32 [12], P('phase'), parts along dimension 0
There are 2 independent parts, one for each index of `phase`. A program takes and returns all parts, laid end to end along the dimension named above; an argument that names none is the same for every part. Nothing has to cross between parts.
Inputs may be any that keep to these rules, and one draw needn't show every extreme that they name: `field_w`: potentials of the two species at each cell. The first three entries are the diagonal of the inverse metric, from 0.7 to 1; the last three are its off-diagonal entries, from -0.25 to 0.25.
All inputs are finite; a program needn't handle non-finite values.
Results may differ from a plain program's by a relative error of at most 0.0003.
Values sent between devices are 32-bit elements; how exact they have to be, the bound alone decides.
No kernel may reach another device: no remote copies, remote signals or barrier semaphores. Data moves between devices by JAX's collectives and lax.ppermute only.
A program may use at most 64 MiB of HBM per device.

v0:
```python
import jax
import jax.numpy as jnp
from jax import lax
from jax.sharding import PartitionSpec as P

ARMS = 16
SPECIES = 2
STEPS = 16


def padded(value, sides, width):
    for axis, dim in sides:
        count, length = (lax.axis_size(axis), value.shape[dim])
        up = [(i, (i + 1) % count) for i in range(count)]
        down = [(j, i) for i, j in up]
        last = lax.slice_in_dim(value, length - width, length, axis=dim)
        initial = lax.slice_in_dim(value, 0, width, axis=dim)
        before = lax.ppermute(last, axis, up)
        after = lax.ppermute(initial, axis, down)
        value = jnp.concatenate([before, value, after], axis=dim)
    return value


def prefix(value, axis, combine, identity, reverse):
    count, here = (lax.axis_size(axis), lax.axis_index(axis))
    everything = lax.all_gather(value, axis)
    start = jnp.broadcast_to(jnp.asarray(identity, value.dtype), value.shape)

    def turn(k, before):
        at = count - 1 - k if reverse else k
        reached = at > here if reverse else at < here
        new = combine(before, everything[at])
        return jnp.where(reached, new, before)

    return lax.fori_loop(0, count, turn, start)


def upward(values, along):
    return jnp.roll(values, -1, along)


def downward(values, along):
    return jnp.roll(values, 1, along)


def differences(centre, plus_x, minus_x):
    second_xx = plus_x + minus_x - 2.0 * centre
    second_yy = upward(centre, 2) + downward(centre, 2) - 2.0 * centre
    second_zz = upward(centre, 3) + downward(centre, 3) - 2.0 * centre
    second_xy = 0.25 * (
        upward(plus_x, 2) - downward(plus_x, 2) - upward(minus_x, 2) + downward(minus_x, 2)
    )
    second_xz = 0.25 * (
        upward(plus_x, 3) - downward(plus_x, 3) - upward(minus_x, 3) + downward(minus_x, 3)
    )
    above_y = upward(centre, 2)
    below_y = downward(centre, 2)
    second_yz = 0.25 * (
        upward(above_y, 3) - downward(above_y, 3) - upward(below_y, 3) + downward(below_y, 3)
    )
    return (second_xx, second_yy, second_zz, second_xy, second_xz, second_yz)


def laplace(seconds, metric):
    diagonal_part = metric[0] * seconds[0] + metric[1] * seconds[1] + metric[2] * seconds[2]
    return diagonal_part + 2.0 * (
        metric[3] * seconds[3] + metric[4] * seconds[4] + metric[5] * seconds[5]
    )


def advance(extended, half_decay, step_size, metric, active):
    scaled = half_decay * extended
    centre = scaled[:, 1:-1]
    seconds = differences(centre, scaled[:, 2:], scaled[:, :-2])
    updated = half_decay[:, 1:-1] * (
        centre + step_size[:, None, None, None] * laplace(seconds, metric)
    )
    return (jnp.where(active[:, None, None, None], updated, extended[:, 1:-1]), seconds)


def species_mix(selector, fields):
    mixed_sum = selector[:, 0, None, None, None] * fields[0][None]
    mixed_sum = mixed_sum + selector[:, 1, None, None, None] * fields[1][None]
    return mixed_sum


def gather_species(selector, per_arm):
    return jnp.stack(
        [
            jnp.sum(selector[:, species, None, None, None] * per_arm, axis=0)
            for species in range(selector.shape[1])
        ]
    )


def exclusive_product(finals):
    lower = jnp.cumprod(finals, axis=0)
    upper = jnp.cumprod(finals[::-1], axis=0)[::-1]
    unity = jnp.ones_like(finals[:1])
    before = jnp.concatenate([unity, lower[:-1]], 0)
    after = jnp.concatenate([upper[1:], unity], 0)
    return (before * after, lower[-1])


def contour_weight(position, arm_counts, step_size):
    ends = jnp.logical_or(position == 0, position == arm_counts)
    return step_size * jnp.where(position > arm_counts, 0.0, jnp.where(ends, 0.5, 1.0))


def multiply(first_part, second_part):
    return first_part * second_part


def extend(values):
    return padded(values, (("slab", 1),), 1)


def local(field_w, metric, arm_length, arm_steps, arm_species):
    slab_cells = field_w.shape[1]
    layers = 1
    profile = (arm_length.shape[0], slab_cells, field_w.shape[2], field_w.shape[3])
    step_size = arm_length / arm_steps.astype(jnp.float32)
    selector = (arm_species[:, None] == jnp.arange(SPECIES, dtype=jnp.int32)[None, :]).astype(
        jnp.float32
    )
    field_ext = padded(field_w, (("slab", 1),), layers)
    half_decay = jnp.exp(-0.5 * step_size[:, None, None, None] * species_mix(selector, field_ext))
    history = jnp.zeros((STEPS + 1,) + profile, jnp.float32)
    history = history.at[0].set(1.0)

    def forward_block(block_index, state_in):
        propagator, history = state_in
        extended = extend(propagator)
        step_index = block_index * layers + 0
        active = step_index >= STEPS - arm_steps
        extended, unused = advance(extended, half_decay, step_size, metric, active)
        history = lax.dynamic_update_index_in_dim(history, extended, step_index + 1, 0)
        return (extended, history)

    propagator, history = lax.fori_loop(
        0, STEPS // layers, forward_block, (jnp.ones(profile, jnp.float32), history)
    )
    excluded, local_total = exclusive_product(propagator)
    lower_part = prefix(local_total, "arm", multiply, jnp.ones_like(local_total), False)
    upper_part = prefix(local_total, "arm", multiply, jnp.ones_like(local_total), True)
    others = lower_part * upper_part
    adjoint = excluded * others[None]
    product_all = local_total * others

    def backward_block(block_index, state_in):
        adjoint_now, density_acc, stress_acc = state_in
        extended = extend(adjoint_now)
        step_index = block_index * layers + 0
        paired = lax.dynamic_index_in_dim(history, STEPS - step_index, 0, keepdims=False)
        weights = contour_weight(step_index, arm_steps, step_size)
        density_acc = (
            density_acc
            + weights[:, None, None, None] * paired * extended[:, layers : layers + slab_cells]
        )
        active = step_index < arm_steps
        extended, seconds = advance(extended, half_decay, step_size, metric, active)
        arm_sums = jnp.stack([jnp.sum(paired * second, axis=(1, 2, 3)) for second in seconds])
        stress_acc = stress_acc + jnp.dot(
            arm_sums, step_size * active.astype(jnp.float32), precision=lax.Precision.HIGHEST
        )
        return (extended, density_acc, stress_acc)

    start_state = (adjoint, jnp.zeros(profile, jnp.float32), jnp.zeros((6,), jnp.float32))
    adjoint, density_acc, stress_acc = lax.fori_loop(
        0, STEPS // layers, backward_block, start_state
    )
    final_weights = contour_weight(STEPS, arm_steps, step_size)
    density_acc = density_acc + final_weights[:, None, None, None] * history[0] * adjoint
    totals = lax.psum((stress_acc, jnp.sum(product_all)), ("slab", "arm"))
    partition = totals[1] / lax.axis_size("arm")
    cell_count = slab_cells * lax.axis_size("slab") * profile[2] * profile[3]
    density_scale = cell_count / (ARMS * partition)
    shares = lax.psum_scatter(
        gather_species(selector, density_acc), "arm", scatter_dimension=2, tiled=True
    )
    return (shares * density_scale, totals[0] / (ARMS * partition))


def solution(mesh):
    return jax.shard_map(
        local,
        mesh=mesh,
        in_specs=(P(None, ("phase", "slab"), None, None), P("phase"), P("arm"), P("arm"), P("arm")),
        out_specs=(P(None, ("phase", "slab"), "arm", None), P("phase")),
        check_vma=False,
    )
```

profile of v0, /device:TPU:0, one launch (start us, length us, event | category | flops | bytes accessed | tf_op | source)
XLA Modules:
  0.0 641.5 jit_solution(15803081879544623338)
XLA Ops:
  8.0 3.0 collective-permute-start.4
  11.0 3.1 collective-permute-start.5
  19.4 9.0 %copy.44 = f32[17,8,4,32,128]{4,3,2,1,0:T(8,128)} copy(f32[17,8,4,32,128]{4,3,2,1,0:T(8,128)} %constant.266.clone.1) | data formatting | bytes 17825792
  28.8 256.5 %while.69 = (s32[]{:T(128)}, f32[8,4,32,128]{3,2,1,0:T(8,128)S(1)}, f32[17,8,4,32,128]{4,3,2,1,0:T(8,128)}, s32[8]{0:T(128)S(1)}, f32[8,6,32,128]{3,2,1,0:T(8,12...) while((s32[]{:T(128)}, f32[8,4,32,128]{3,2,1,0:T(8,128)S(1)}, ...), condition=%wide.region_1.2_spmd.clone, body=%wide.region_0.0_spmd.clone.sunk | while | flops 7667734 | bytes 33820016 | solution.py:140
  33.9 4.7 collective-permute-done.1
  41.3 5.2 bitcast_dynamic-update-slice_fusion.2
  49.3 3.4 collective-permute-done
  58.1 5.2 bitcast_dynamic-update-slice_fusion.2
  66.1 3.1 collective-permute-done
  73.9 5.2 bitcast_dynamic-update-slice_fusion.2
  89.7 5.2 bitcast_dynamic-update-slice_fusion.2
  105.5 5.2 bitcast_dynamic-update-slice_fusion.2
  121.3 5.2 bitcast_dynamic-update-slice_fusion.2
  137.1 5.2 bitcast_dynamic-update-slice_fusion.2
  152.9 5.2 bitcast_dynamic-update-slice_fusion.2
  168.7 5.2 bitcast_dynamic-update-slice_fusion.2
  184.5 5.2 bitcast_dynamic-update-slice_fusion.2
  200.3 5.2 bitcast_dynamic-update-slice_fusion.2
  216.1 5.2 bitcast_dynamic-update-slice_fusion.2
  231.9 5.2 bitcast_dynamic-update-slice_fusion.2
  242.2 2.9 collective-permute-done.1
  247.8 5.2 bitcast_dynamic-update-slice_fusion.2
  258.3 3.2 collective-permute-done.1
  264.3 5.2 bitcast_dynamic-update-slice_fusion.2
  280.1 5.2 bitcast_dynamic-update-slice_fusion.2
  290.6 309.1 %while.72 = (s32[]{:T(128)}, f32[8,4,32,128]{3,2,1,0:T(8,128)S(1)}, f32[8,4,32,128]{3,2,1,0:T(8,128)}, f32[6]{0:T(128)S(1)}, s32[8]{0:T(128)S(1)}, /*index=5*/f3...) while((s32[]{:T(128)}, f32[8,4,32,128]{3,2,1,0:T(8,128)S(1)}, ...), condition=%wide.region_15.16_spmd.clone, body=%wide.region_8.15_spmd.clone.sunk | while | flops 10289763 | bytes 41682308 | solution.py:169
  301.8 4.2 fusion.133
  306.2 3.7 multiply_select_fusion.8
  321.5 4.2 fusion.133
  325.9 3.7 multiply_select_fusion.8
  334.7 4.2 collective-permute-done.3
  341.6 4.2 fusion.133
  346.0 3.7 multiply_select_fusion.8
  354.8 4.2 collective-permute-done.3
  361.8 4.2 fusion.133
  366.2 3.7 multiply_select_fusion.8
  375.0 4.0 collective-permute-done.3
  381.8 4.2 fusion.133
  386.2 3.7 multiply_select_fusion.8
  400.7 4.2 fusion.133
  405.1 3.7 multiply_select_fusion.8
  419.5 4.2 fusion.133
  423.9 3.7 multiply_select_fusion.8
  432.7 3.3 collective-permute-done.3
  438.8 4.2 fusion.133
  443.2 3.7 multiply_select_fusion.8
  452.1 4.8 collective-permute-done.3
  459.8 4.2 fusion.133
  464.2 3.7 multiply_select_fusion.8
  478.6 4.2 fusion.133
  483.0 3.7 multiply_select_fusion.8
  497.5 4.2 fusion.133
  501.9 3.7 multiply_select_fusion.8
  516.3 4.2 fusion.133
  520.7 3.7 multiply_select_fusion.8
  535.1 4.2 fusion.133
  539.5 3.7 multiply_select_fusion.8
  554.1 4.2 fusion.133
  558.5 3.7 multiply_select_fusion.8
  572.8 4.2 fusion.133
  577.2 3.7 multiply_select_fusion.8
  591.6 4.2 fusion.133
  596.0 3.7 multiply_select_fusion.8
  601.8 30.1 %all-reduce.2 = (f32[]{:T(128)}, f32[6]{0:T(128)S(1)}) all-reduce(f32[]{:T(128)} %get-tuple-element.820, f32[6]{0:T(128)S(1)} %get-tuple-element.640), channel_id=1, replica_groups=mesh['phase'=2,'slab'=8,'arm'=2] {'slab','arm'}, use_global_device_ids=true, to_apply=%region_20.21 | all-reduce | flops 7 | bytes 56 | tf_op jit(solution)/shard_map/psum | solution.py:174
  (567 shorter events, 328.7 us)
Async XLA Ops:
  7.2 626.0 %reduce-scatter.2.cloned.1.call-start = ((), (), s32[]{:S(2)}) async-start(), calls=%async_computation.1 | async-start | bytes 196608 | tf_op jit(solution)/shard_map/reduce_scatter | solution.py:178
  8.0 20.4 %collective-permute-start.4 = (f32[2,1,32,128]{3,2,1,0:T(8,128)S(1)}, f32[2,1,32,128]{3,2,1,0:T(8,128)S(1)}, u32[]{:S(2)}, u32[]{:S(2)}) collective-permute-start(f32[2,1,32,128]{3,2,1,0:T(8,128)S(1)} %get-tuple-element.909), channel_id=1, source_target_pairs={{0,2},{2,4},{4,6},{6,8},{8,10},{10,12},{12,14},{14,0},{1,3},{3,5},... | collective-permute-start | bytes 98312 | tf_op jit(solution)/shard_map/ppermute | solution.py:18
  11.0 17.5 %collective-permute-start.5 = (f32[2,1,32,128]{3,2,1,0:T(8,128)S(1)}, f32[2,1,32,128]{3,2,1,0:T(8,128)S(1)}, u32[]{:S(2)}, u32[]{:S(2)}) collective-permute-start(f32[2,1,32,128]{3,2,1,0:T(8,128)S(1)} %get-tuple-element.908), channel_id=1, source_target_pairs={{2,0},{4,2},{6,4},{8,6},{10,8},{12,10},{14,12},{0,14},{3,1},{5,3},... | collective-permute-start | bytes 98312 | tf_op jit(solution)/shard_map/ppermute | solution.py:19
  28.8 5.0 collective-permute-start
  30.9 7.7 %collective-permute-start.1 = (f32[8,1,32,128]{3,2,1,0:T(8,128)S(1)}, f32[8,1,32,128]{3,2,1,0:T(8,128)S(1)}, u32[]{:S(2)}, u32[]{:S(2)}) collective-permute-start(f32[8,1,32,128]{3,2,1,0:T(8,128)S(1)} %get-tuple-element.1167), channel_id=1, source_target_pairs={{0,2},{2,4},{4,6},{6,8},{8,10},{10,12},{12,14},{14,0},{1,3},{3,5},... | collective-permute-start | bytes 393224 | tf_op jit(solution)/shard_map/while/body/eval_jaxpr/ppermute | solution.py:18
  46.5 6.1 collective-permute-start
  47.7 7.7 %collective-permute-start.1 = (f32[8,1,32,128]{3,2,1,0:T(8,128)S(1)}, f32[8,1,32,128]{3,2,1,0:T(8,128)S(1)}, u32[]{:S(2)}, u32[]{:S(2)}) collective-permute-start(f32[8,1,32,128]{3,2,1,0:T(8,128)S(1)} %get-tuple-element.1167), channel_id=1, source_target_pairs={{0,2},{2,4},{4,6},{6,8},{8,10},{10,12},{12,14},{14,0},{1,3},{3,5},... | collective-permute-start | bytes 393224 | tf_op jit(solution)/shard_map/while/body/eval_jaxpr/ppermute | solution.py:18
  63.4 5.8 collective-permute-start
  63.5 7.7 %collective-permute-start.1 = (f32[8,1,32,128]{3,2,1,0:T(8,128)S(1)}, f32[8,1,32,128]{3,2,1,0:T(8,128)S(1)}, u32[]{:S(2)}, u32[]{:S(2)}) collective-permute-start(f32[8,1,32,128]{3,2,1,0:T(8,128)S(1)} %get-tuple-element.1167), channel_id=1, source_target_pairs={{0,2},{2,4},{4,6},{6,8},{8,10},{10,12},{12,14},{14,0},{1,3},{3,5},... | collective-permute-start | bytes 393224 | tf_op jit(solution)/shard_map/while/body/eval_jaxpr/ppermute | solution.py:18
  79.2 5.0 collective-permute-start
  79.2 7.7 %collective-permute-start.1 = (f32[8,1,32,128]{3,2,1,0:T(8,128)S(1)}, f32[8,1,32,128]{3,2,1,0:T(8,128)S(1)}, u32[]{:S(2)}, u32[]{:S(2)}) collective-permute-start(f32[8,1,32,128]{3,2,1,0:T(8,128)S(1)} %get-tuple-element.1167), channel_id=1, source_target_pairs={{0,2},{2,4},{4,6},{6,8},{8,10},{10,12},{12,14},{14,0},{1,3},{3,5},... | collective-permute-start | bytes 393224 | tf_op jit(solution)/shard_map/while/body/eval_jaxpr/ppermute | solution.py:18
  95.0 5.0 collective-permute-start
  95.0 7.7 %collective-permute-start.1 = (f32[8,1,32,128]{3,2,1,0:T(8,128)S(1)}, f32[8,1,32,128]{3,2,1,0:T(8,128)S(1)}, u32[]{:S(2)}, u32[]{:S(2)}) collective-permute-start(f32[8,1,32,128]{3,2,1,0:T(8,128)S(1)} %get-tuple-element.1167), channel_id=1, source_target_pairs={{0,2},{2,4},{4,6},{6,8},{8,10},{10,12},{12,14},{14,0},{1,3},{3,5},... | collective-permute-start | bytes 393224 | tf_op jit(solution)/shard_map/while/body/eval_jaxpr/ppermute | solution.py:18
  110.8 5.0 collective-permute-start
  110.8 7.7 %collective-permute-start.1 = (f32[8,1,32,128]{3,2,1,0:T(8,128)S(1)}, f32[8,1,32,128]{3,2,1,0:T(8,128)S(1)}, u32[]{:S(2)}, u32[]{:S(2)}) collective-permute-start(f32[8,1,32,128]{3,2,1,0:T(8,128)S(1)} %get-tuple-element.1167), channel_id=1, source_target_pairs={{0,2},{2,4},{4,6},{6,8},{8,10},{10,12},{12,14},{14,0},{1,3},{3,5},... | collective-permute-start | bytes 393224 | tf_op jit(solution)/shard_map/while/body/eval_jaxpr/ppermute | solution.py:18
  126.5 5.0 collective-permute-start
  126.6 7.7 %collective-permute-start.1 = (f32[8,1,32,128]{3,2,1,0:T(8,128)S(1)}, f32[8,1,32,128]{3,2,1,0:T(8,128)S(1)}, u32[]{:S(2)}, u32[]{:S(2)}) collective-permute-start(f32[8,1,32,128]{3,2,1,0:T(8,128)S(1)} %get-tuple-element.1167), channel_id=1, source_target_pairs={{0,2},{2,4},{4,6},{6,8},{8,10},{10,12},{12,14},{14,0},{1,3},{3,5},... | collective-permute-start | bytes 393224 | tf_op jit(solution)/shard_map/while/body/eval_jaxpr/ppermute | solution.py:18
  142.3 5.0 collective-permute-start
  142.4 7.7 %collective-permute-start.1 = (f32[8,1,32,128]{3,2,1,0:T(8,128)S(1)}, f32[8,1,32,128]{3,2,1,0:T(8,128)S(1)}, u32[]{:S(2)}, u32[]{:S(2)}) collective-permute-start(f32[8,1,32,128]{3,2,1,0:T(8,128)S(1)} %get-tuple-element.1167), channel_id=1, source_target_pairs={{0,2},{2,4},{4,6},{6,8},{8,10},{10,12},{12,14},{14,0},{1,3},{3,5},... | collective-permute-start | bytes 393224 | tf_op jit(solution)/shard_map/while/body/eval_jaxpr/ppermute | solution.py:18
  158.1 5.0 collective-permute-start
  158.2 7.7 %collective-permute-start.1 = (f32[8,1,32,128]{3,2,1,0:T(8,128)S(1)}, f32[8,1,32,128]{3,2,1,0:T(8,128)S(1)}, u32[]{:S(2)}, u32[]{:S(2)}) collective-permute-start(f32[8,1,32,128]{3,2,1,0:T(8,128)S(1)} %get-tuple-element.1167), channel_id=1, source_target_pairs={{0,2},{2,4},{4,6},{6,8},{8,10},{10,12},{12,14},{14,0},{1,3},{3,5},... | collective-permute-start | bytes 393224 | tf_op jit(solution)/shard_map/while/body/eval_jaxpr/ppermute | solution.py:18
  174.0 5.0 collective-permute-start
  174.0 7.7 %collective-permute-start.1 = (f32[8,1,32,128]{3,2,1,0:T(8,128)S(1)}, f32[8,1,32,128]{3,2,1,0:T(8,128)S(1)}, u32[]{:S(2)}, u32[]{:S(2)}) collective-permute-start(f32[8,1,32,128]{3,2,1,0:T(8,128)S(1)} %get-tuple-element.1167), channel_id=1, source_target_pairs={{0,2},{2,4},{4,6},{6,8},{8,10},{10,12},{12,14},{14,0},{1,3},{3,5},... | collective-permute-start | bytes 393224 | tf_op jit(solution)/shard_map/while/body/eval_jaxpr/ppermute | solution.py:18
  189.7 5.0 collective-permute-start
  189.8 7.7 %collective-permute-start.1 = (f32[8,1,32,128]{3,2,1,0:T(8,128)S(1)}, f32[8,1,32,128]{3,2,1,0:T(8,128)S(1)}, u32[]{:S(2)}, u32[]{:S(2)}) collective-permute-start(f32[8,1,32,128]{3,2,1,0:T(8,128)S(1)} %get-tuple-element.1167), channel_id=1, source_target_pairs={{0,2},{2,4},{4,6},{6,8},{8,10},{10,12},{12,14},{14,0},{1,3},{3,5},... | collective-permute-start | bytes 393224 | tf_op jit(solution)/shard_map/while/body/eval_jaxpr/ppermute | solution.py:18
  205.5 5.0 collective-permute-start
  205.6 7.7 %collective-permute-start.1 = (f32[8,1,32,128]{3,2,1,0:T(8,128)S(1)}, f32[8,1,32,128]{3,2,1,0:T(8,128)S(1)}, u32[]{:S(2)}, u32[]{:S(2)}) collective-permute-start(f32[8,1,32,128]{3,2,1,0:T(8,128)S(1)} %get-tuple-element.1167), channel_id=1, source_target_pairs={{0,2},{2,4},{4,6},{6,8},{8,10},{10,12},{12,14},{14,0},{1,3},{3,5},... | collective-permute-start | bytes 393224 | tf_op jit(solution)/shard_map/while/body/eval_jaxpr/ppermute | solution.py:18
  221.3 5.0 collective-permute-start
  221.4 7.8 %collective-permute-start.1 = (f32[8,1,32,128]{3,2,1,0:T(8,128)S(1)}, f32[8,1,32,128]{3,2,1,0:T(8,128)S(1)}, u32[]{:S(2)}, u32[]{:S(2)}) collective-permute-start(f32[8,1,32,128]{3,2,1,0:T(8,128)S(1)} %get-tuple-element.1167), channel_id=1, source_target_pairs={{0,2},{2,4},{4,6},{6,8},{8,10},{10,12},{12,14},{14,0},{1,3},{3,5},... | collective-permute-start | bytes 393224 | tf_op jit(solution)/shard_map/while/body/eval_jaxpr/ppermute | solution.py:18
  237.2 5.0 collective-permute-start
  237.3 7.8 %collective-permute-start.1 = (f32[8,1,32,128]{3,2,1,0:T(8,128)S(1)}, f32[8,1,32,128]{3,2,1,0:T(8,128)S(1)}, u32[]{:S(2)}, u32[]{:S(2)}) collective-permute-start(f32[8,1,32,128]{3,2,1,0:T(8,128)S(1)} %get-tuple-element.1167), channel_id=1, source_target_pairs={{0,2},{2,4},{4,6},{6,8},{8,10},{10,12},{12,14},{14,0},{1,3},{3,5},... | collective-permute-start | bytes 393224 | tf_op jit(solution)/shard_map/while/body/eval_jaxpr/ppermute | solution.py:18
  253.1 5.2 collective-permute-start
  253.2 8.4 %collective-permute-start.1 = (f32[8,1,32,128]{3,2,1,0:T(8,128)S(1)}, f32[8,1,32,128]{3,2,1,0:T(8,128)S(1)}, u32[]{:S(2)}, u32[]{:S(2)}) collective-permute-start(f32[8,1,32,128]{3,2,1,0:T(8,128)S(1)} %get-tuple-element.1167), channel_id=1, source_target_pairs={{0,2},{2,4},{4,6},{6,8},{8,10},{10,12},{12,14},{14,0},{1,3},{3,5},... | collective-permute-start | bytes 393224 | tf_op jit(solution)/shard_map/while/body/eval_jaxpr/ppermute | solution.py:18
  269.6 5.5 collective-permute-start
  269.6 7.7 %collective-permute-start.1 = (f32[8,1,32,128]{3,2,1,0:T(8,128)S(1)}, f32[8,1,32,128]{3,2,1,0:T(8,128)S(1)}, u32[]{:S(2)}, u32[]{:S(2)}) collective-permute-start(f32[8,1,32,128]{3,2,1,0:T(8,128)S(1)} %get-tuple-element.1167), channel_id=1, source_target_pairs={{0,2},{2,4},{4,6},{6,8},{8,10},{10,12},{12,14},{14,0},{1,3},{3,5},... | collective-permute-start | bytes 393224 | tf_op jit(solution)/shard_map/while/body/eval_jaxpr/ppermute | solution.py:18
  290.6 5.6 collective-permute-start.2
  290.7 8.4 %collective-permute-start.3 = (f32[8,1,32,128]{3,2,1,0:T(8,128)S(1)}, f32[8,1,32,128]{3,2,1,0:T(8,128)S(1)}, u32[]{:S(2)}, u32[]{:S(2)}) collective-permute-start(f32[8,1,32,128]{3,2,1,0:T(8,128)S(1)} %get-tuple-element.1226), channel_id=1, source_target_pairs={{0,2},{2,4},{4,6},{6,8},{8,10},{10,12},{12,14},{14,0},{1,3},{3,5},... | collective-permute-start | bytes 393224 | tf_op jit(solution)/shard_map/while/body/eval_jaxpr/ppermute | solution.py:18
  310.0 6.5 %collective-permute-start.2 = (f32[8,1,32,128]{3,2,1,0:T(8,128)S(1)}, f32[8,1,32,128]{3,2,1,0:T(8,128)S(1)}, u32[]{:S(2)}, u32[]{:S(2)}) collective-permute-start(f32[8,1,32,128]{3,2,1,0:T(8,128)S(1)} %get-tuple-element.1225), channel_id=1, source_target_pairs={{2,0},{4,2},{6,4},{8,6},{10,8},{12,10},{14,12},{0,14},{3,1},{5,3},... | collective-permute-start | bytes 393224 | tf_op jit(solution)/shard_map/while/body/eval_jaxpr/ppermute | solution.py:19
  311.0 7.7 %collective-permute-start.3 = (f32[8,1,32,128]{3,2,1,0:T(8,128)S(1)}, f32[8,1,32,128]{3,2,1,0:T(8,128)S(1)}, u32[]{:S(2)}, u32[]{:S(2)}) collective-permute-start(f32[8,1,32,128]{3,2,1,0:T(8,128)S(1)} %get-tuple-element.1226), channel_id=1, source_target_pairs={{0,2},{2,4},{4,6},{6,8},{8,10},{10,12},{12,14},{14,0},{1,3},{3,5},... | collective-permute-start | bytes 393224 | tf_op jit(solution)/shard_map/while/body/eval_jaxpr/ppermute | solution.py:18
  329.7 5.0 collective-permute-start.2
  331.2 7.7 %collective-permute-start.3 = (f32[8,1,32,128]{3,2,1,0:T(8,128)S(1)}, f32[8,1,32,128]{3,2,1,0:T(8,128)S(1)}, u32[]{:S(2)}, u32[]{:S(2)}) collective-permute-start(f32[8,1,32,128]{3,2,1,0:T(8,128)S(1)} %get-tuple-element.1226), channel_id=1, source_target_pairs={{0,2},{2,4},{4,6},{6,8},{8,10},{10,12},{12,14},{14,0},{1,3},{3,5},... | collective-permute-start | bytes 393224 | tf_op jit(solution)/shard_map/while/body/eval_jaxpr/ppermute | solution.py:18
  351.3 7.7 %collective-permute-start.3 = (f32[8,1,32,128]{3,2,1,0:T(8,128)S(1)}, f32[8,1,32,128]{3,2,1,0:T(8,128)S(1)}, u32[]{:S(2)}, u32[]{:S(2)}) collective-permute-start(f32[8,1,32,128]{3,2,1,0:T(8,128)S(1)} %get-tuple-element.1226), channel_id=1, source_target_pairs={{0,2},{2,4},{4,6},{6,8},{8,10},{10,12},{12,14},{14,0},{1,3},{3,5},... | collective-permute-start | bytes 393224 | tf_op jit(solution)/shard_map/while/body/eval_jaxpr/ppermute | solution.py:18
  371.3 7.7 %collective-permute-start.3 = (f32[8,1,32,128]{3,2,1,0:T(8,128)S(1)}, f32[8,1,32,128]{3,2,1,0:T(8,128)S(1)}, u32[]{:S(2)}, u32[]{:S(2)}) collective-permute-start(f32[8,1,32,128]{3,2,1,0:T(8,128)S(1)} %get-tuple-element.1226), channel_id=1, source_target_pairs={{0,2},{2,4},{4,6},{6,8},{8,10},{10,12},{12,14},{14,0},{1,3},{3,5},... | collective-permute-start | bytes 393224 | tf_op jit(solution)/shard_map/while/body/eval_jaxpr/ppermute | solution.py:18
  390.0 6.3 collective-permute-start.2
  390.2 7.7 %collective-permute-start.3 = (f32[8,1,32,128]{3,2,1,0:T(8,128)S(1)}, f32[8,1,32,128]{3,2,1,0:T(8,128)S(1)}, u32[]{:S(2)}, u32[]{:S(2)}) collective-permute-start(f32[8,1,32,128]{3,2,1,0:T(8,128)S(1)} %get-tuple-element.1226), channel_id=1, source_target_pairs={{0,2},{2,4},{4,6},{6,8},{8,10},{10,12},{12,14},{14,0},{1,3},{3,5},... | collective-permute-start | bytes 393224 | tf_op jit(solution)/shard_map/while/body/eval_jaxpr/ppermute | solution.py:18
  408.8 5.4 collective-permute-start.2
  409.0 7.7 %collective-permute-start.3 = (f32[8,1,32,128]{3,2,1,0:T(8,128)S(1)}, f32[8,1,32,128]{3,2,1,0:T(8,128)S(1)}, u32[]{:S(2)}, u32[]{:S(2)}) collective-permute-start(f32[8,1,32,128]{3,2,1,0:T(8,128)S(1)} %get-tuple-element.1226), channel_id=1, source_target_pairs={{0,2},{2,4},{4,6},{6,8},{8,10},{10,12},{12,14},{14,0},{1,3},{3,5},... | collective-permute-start | bytes 393224 | tf_op jit(solution)/shard_map/while/body/eval_jaxpr/ppermute | solution.py:18
  427.6 5.0 collective-permute-start.2
  428.3 7.7 %collective-permute-start.3 = (f32[8,1,32,128]{3,2,1,0:T(8,128)S(1)}, f32[8,1,32,128]{3,2,1,0:T(8,128)S(1)}, u32[]{:S(2)}, u32[]{:S(2)}) collective-permute-start(f32[8,1,32,128]{3,2,1,0:T(8,128)S(1)} %get-tuple-element.1226), channel_id=1, source_target_pairs={{0,2},{2,4},{4,6},{6,8},{8,10},{10,12},{12,14},{14,0},{1,3},{3,5},... | collective-permute-start | bytes 393224 | tf_op jit(solution)/shard_map/while/body/eval_jaxpr/ppermute | solution.py:18
  447.0 5.2 collective-permute-start.2
  449.3 7.7 %collective-permute-start.3 = (f32[8,1,32,128]{3,2,1,0:T(8,128)S(1)}, f32[8,1,32,128]{3,2,1,0:T(8,128)S(1)}, u32[]{:S(2)}, u32[]{:S(2)}) collective-permute-start(f32[8,1,32,128]{3,2,1,0:T(8,128)S(1)} %get-tuple-element.1226), channel_id=1, source_target_pairs={{0,2},{2,4},{4,6},{6,8},{8,10},{10,12},{12,14},{14,0},{1,3},{3,5},... | collective-permute-start | bytes 393224 | tf_op jit(solution)/shard_map/while/body/eval_jaxpr/ppermute | solution.py:18
  467.9 6.4 %collective-permute-start.2 = (f32[8,1,32,128]{3,2,1,0:T(8,128)S(1)}, f32[8,1,32,128]{3,2,1,0:T(8,128)S(1)}, u32[]{:S(2)}, u32[]{:S(2)}) collective-permute-start(f32[8,1,32,128]{3,2,1,0:T(8,128)S(1)} %get-tuple-element.1225), channel_id=1, source_target_pairs={{2,0},{4,2},{6,4},{8,6},{10,8},{12,10},{14,12},{0,14},{3,1},{5,3},... | collective-permute-start | bytes 393224 | tf_op jit(solution)/shard_map/while/body/eval_jaxpr/ppermute | solution.py:19
  468.2 7.7 %collective-permute-start.3 = (f32[8,1,32,128]{3,2,1,0:T(8,128)S(1)}, f32[8,1,32,128]{3,2,1,0:T(8,128)S(1)}, u32[]{:S(2)}, u32[]{:S(2)}) collective-permute-start(f32[8,1,32,128]{3,2,1,0:T(8,128)S(1)} %get-tuple-element.1226), channel_id=1, source_target_pairs={{0,2},{2,4},{4,6},{6,8},{8,10},{10,12},{12,14},{14,0},{1,3},{3,5},... | collective-permute-start | bytes 393224 | tf_op jit(solution)/shard_map/while/body/eval_jaxpr/ppermute | solution.py:18
  486.8 5.6 collective-permute-start.2
  487.1 7.7 %collective-permute-start.3 = (f32[8,1,32,128]{3,2,1,0:T(8,128)S(1)}, f32[8,1,32,128]{3,2,1,0:T(8,128)S(1)}, u32[]{:S(2)}, u32[]{:S(2)}) collective-permute-start(f32[8,1,32,128]{3,2,1,0:T(8,128)S(1)} %get-tuple-element.1226), channel_id=1, source_target_pairs={{0,2},{2,4},{4,6},{6,8},{8,10},{10,12},{12,14},{14,0},{1,3},{3,5},... | collective-permute-start | bytes 393224 | tf_op jit(solution)/shard_map/while/body/eval_jaxpr/ppermute | solution.py:18
  505.7 5.0 collective-permute-start.2
  505.8 7.7 %collective-permute-start.3 = (f32[8,1,32,128]{3,2,1,0:T(8,128)S(1)}, f32[8,1,32,128]{3,2,1,0:T(8,128)S(1)}, u32[]{:S(2)}, u32[]{:S(2)}) collective-permute-start(f32[8,1,32,128]{3,2,1,0:T(8,128)S(1)} %get-tuple-element.1226), channel_id=1, source_target_pairs={{0,2},{2,4},{4,6},{6,8},{8,10},{10,12},{12,14},{14,0},{1,3},{3,5},... | collective-permute-start | bytes 393224 | tf_op jit(solution)/shard_map/while/body/eval_jaxpr/ppermute | solution.py:18
  524.5 6.4 %collective-permute-start.2 = (f32[8,1,32,128]{3,2,1,0:T(8,128)S(1)}, f32[8,1,32,128]{3,2,1,0:T(8,128)S(1)}, u32[]{:S(2)}, u32[]{:S(2)}) collective-permute-start(f32[8,1,32,128]{3,2,1,0:T(8,128)S(1)} %get-tuple-element.1225), channel_id=1, source_target_pairs={{2,0},{4,2},{6,4},{8,6},{10,8},{12,10},{14,12},{0,14},{3,1},{5,3},... | collective-permute-start | bytes 393224 | tf_op jit(solution)/shard_map/while/body/eval_jaxpr/ppermute | solution.py:19
  524.5 7.8 %collective-permute-start.3 = (f32[8,1,32,128]{3,2,1,0:T(8,128)S(1)}, f32[8,1,32,128]{3,2,1,0:T(8,128)S(1)}, u32[]{:S(2)}, u32[]{:S(2)}) collective-permute-start(f32[8,1,32,128]{3,2,1,0:T(8,128)S(1)} %get-tuple-element.1226), channel_id=1, source_target_pairs={{0,2},{2,4},{4,6},{6,8},{8,10},{10,12},{12,14},{14,0},{1,3},{3,5},... | collective-permute-start | bytes 393224 | tf_op jit(solution)/shard_map/while/body/eval_jaxpr/ppermute | solution.py:18
  543.3 5.6 collective-permute-start.2
  543.6 7.7 %collective-permute-start.3 = (f32[8,1,32,128]{3,2,1,0:T(8,128)S(1)}, f32[8,1,32,128]{3,2,1,0:T(8,128)S(1)}, u32[]{:S(2)}, u32[]{:S(2)}) collective-permute-start(f32[8,1,32,128]{3,2,1,0:T(8,128)S(1)} %get-tuple-element.1226), channel_id=1, source_target_pairs={{0,2},{2,4},{4,6},{6,8},{8,10},{10,12},{12,14},{14,0},{1,3},{3,5},... | collective-permute-start | bytes 393224 | tf_op jit(solution)/shard_map/while/body/eval_jaxpr/ppermute | solution.py:18
  562.3 7.7 %collective-permute-start.3 = (f32[8,1,32,128]{3,2,1,0:T(8,128)S(1)}, f32[8,1,32,128]{3,2,1,0:T(8,128)S(1)}, u32[]{:S(2)}, u32[]{:S(2)}) collective-permute-start(f32[8,1,32,128]{3,2,1,0:T(8,128)S(1)} %get-tuple-element.1226), channel_id=1, source_target_pairs={{0,2},{2,4},{4,6},{6,8},{8,10},{10,12},{12,14},{14,0},{1,3},{3,5},... | collective-permute-start | bytes 393224 | tf_op jit(solution)/shard_map/while/body/eval_jaxpr/ppermute | solution.py:18
  581.0 5.0 collective-permute-start.2
  581.0 7.7 %collective-permute-start.3 = (f32[8,1,32,128]{3,2,1,0:T(8,128)S(1)}, f32[8,1,32,128]{3,2,1,0:T(8,128)S(1)}, u32[]{:S(2)}, u32[]{:S(2)}) collective-permute-start(f32[8,1,32,128]{3,2,1,0:T(8,128)S(1)} %get-tuple-element.1226), channel_id=1, source_target_pairs={{0,2},{2,4},{4,6},{6,8},{8,10},{10,12},{12,14},{14,0},{1,3},{3,5},... | collective-permute-start | bytes 393224 | tf_op jit(solution)/shard_map/while/body/eval_jaxpr/ppermute | solution.py:18
  (7 other events, 352.0 us)
Sparse Core Ops, SparseCore 0:
  601.9 4.8 reduce-scatter.1
where the time goes:
time: 644 us; the launch traced here: 641 us
  other arithmetic  291 us (45%)
  waiting for transfers between devices  140 us (22%)
  local copies, waits for them, and re-layouts  83.4 us (13%)
  starting transfers between devices  73.3 us (11%)
  blocking collectives  32 us (5%)
  between operations  16.8 us (3%)
    ppermute x33, waiting for transfers between devices, padded(): before = lax.ppermute(last, axis, up)  90.8 us
    dynamic_update_slice x16, other arithmetic, forward_block(): lax.dynamic_update_index_in_dim(history, extended, step_index + 1, 0)  82.9 us
    reduce_sum x16, other arithmetic, backward_block(): jnp.sum(paired * second, axis=(1, 2, 3))  67.8 us
    select_n x16, other arithmetic, advance(): jnp.where(active[:, None, None, None], updated, extended[:, 1:-1])  59.6 us
    ppermute x33, starting transfers between devices, padded(): before = lax.ppermute(last, axis, up)  56.1 us
    slice x128, local copies, waits for them, and re-layouts, upward(): return jnp.roll(values, -1, along)  50.9 us
    ppermute x33, waiting for transfers between devices, padded(): after = lax.ppermute(initial, axis, down)  48.9 us
    add x16, other arithmetic, backward_block(): density_acc + weights[:, None, None, None] * paired * extended[:, layers:...  34.6 us
  transfers between devices with their start and end apart: 67, of which 63 were waited for; matrix products, arithmetic and copies ran while one was open for 11% of the time, Pallas kernels for 0%

commit v1 on v0

v1 whole, which is shorter than its diff:
```python
import functools

import jax
import jax.numpy as jnp
from jax import lax
from jax.experimental import pallas as pl
from jax.experimental.pallas import tpu as pltpu
from jax.sharding import PartitionSpec as P

STEPS = 16
ROWS = 8
PLANES = 8


def up_y(parts):
    return parts[1:] + [pltpu.roll(parts[0], ROWS - 1, 0)]


def down_y(parts):
    return [pltpu.roll(parts[-1], 1, 0)] + parts[:-1]


def up_z(value):
    return pltpu.roll(value, value.shape[1] - 1, 1)


def down_z(value):
    return pltpu.roll(value, 1, 1)


def splat(scalar, lanes):
    return jnp.full((ROWS, lanes), scalar, jnp.float32)


def coefficients(arm, lanes, length_ref, steps_ref, metric_ref):
    mu = splat(length_ref[arm], lanes) / splat(steps_ref[arm].astype(jnp.float32), lanes)
    return mu, [mu * metric_ref[k] for k in range(6)]


def blocks(planes):
    size = PLANES if planes % PLANES == 0 else 1
    return planes // size, size


def forward_kernel(arms, length_ref, steps_ref, metric_ref, field_ref, hist_ref, half_ref, keep_ref, give_ref):
    _, planes, parts, _, lanes = hist_ref.shape
    slabs, depth = field_ref.shape[:2]
    arm, core = lax.rem(lax.axis_index("slab"), arms), lax.axis_index("arm")
    count = steps_ref[arm]
    mu, scaled = coefficients(arm, lanes, length_ref, steps_ref, metric_ref)
    c_x, c_y, c_z = scaled[:3]
    c_xy, c_xz, c_yz = (0.5 * s for s in scaled[3:])
    c_0 = 1.0 - 2.0 * (c_x + c_y + c_z)
    decay = -0.5 * mu

    @pl.loop(0, slabs)
    def _(slab):
        for i in range(depth):
            for j in range(parts):
                value = field_ref[slab, i, pl.ds(j, ROWS, stride=parts), :]
                half_ref[slab * depth + i, j] = jnp.exp(decay * value)
                hist_ref[0, slab * depth + i, j] = jnp.ones((ROWS, lanes), jnp.float32)

    trips, size = blocks(planes)

    @pl.loop(0, count)
    def _(step):
        def plane(x):
            x = lax.rem(x, planes)
            half = [half_ref[x, j] for j in range(parts)]
            return half, [half[j] * hist_ref[step, x, j] for j in range(parts)]

        def block(trip, carry):
            minus, centre, half = carry
            first = trip * size
            for i in range(size):
                next_half, plus = plane(first + i + 1)
                diff = [p - m for p, m in zip(plus, minus)]
                total = [p + m for p, m in zip(plus, minus)]
                above, below = up_y(centre), down_y(centre)
                diff_above, diff_below = up_y(diff), down_y(diff)
                for j in range(parts):
                    skew = c_xz * diff[j] + c_yz * (above[j] - below[j])
                    main = c_z * centre[j]
                    value = (
                        c_0 * centre[j]
                        + c_x * total[j]
                        + c_y * (above[j] + below[j])
                        + c_xy * (diff_above[j] - diff_below[j])
                        + (up_z(main + skew) + down_z(main - skew))
                    )
                    hist_ref[step + 1, first + i, j] = half[j] * value
                minus, centre, half = centre, plus, next_half
            return minus, centre, half

        _, before = plane(planes - 1)
        half, here = plane(0)
        lax.fori_loop(0, trips, block, (before, here, half))

    split = parts // 2

    @pl.loop(0, planes)
    def _(x):
        for j in range(split):
            keep_ref[x, j] = hist_ref[count, x, core * split + j]
            give_ref[x, j] = hist_ref[count, x, (1 - core) * split + j]


def exclusive_kernel(arms, pairs_ref, out_ref):
    slabs, rows, _ = pairs_ref.shape

    @pl.loop(0, rows // ROWS)
    def _(block):
        at = pl.ds(pl.multiple_of(block * ROWS, ROWS), ROWS)
        values = [pairs_ref[a, at, :] for a in range(arms)]
        before, after = [None] * arms, [None] * arms
        for a in range(1, arms):
            before[a] = values[a - 1] if before[a - 1] is None else before[a - 1] * values[a - 1]
            b = arms - 1 - a
            after[b] = values[b + 1] if after[b + 1] is None else after[b + 1] * values[b + 1]
        for a in range(arms):
            sides = [s for s in (before[a], after[a]) if s is not None]
            result = sides[0] * sides[1] if len(sides) == 2 else sides[0]
            for copy in range(a, slabs, arms):
                out_ref[copy, at, :] = result


def adjoint_kernel(
    arms, length_ref, steps_ref, species_ref, metric_ref, hist_ref, half_ref, mine_ref, other_ref, out_ref,
    state_ref, square_ref, density_ref, line_ref, tail_ref,
):
    _, planes, parts, _, lanes = hist_ref.shape
    arm, core = lax.rem(lax.axis_index("slab"), arms), lax.axis_index("arm")
    count = steps_ref[arm]
    mu, scaled = coefficients(arm, lanes, length_ref, steps_ref, metric_ref)
    c_x, c_y, c_z = scaled[:3]
    c_xy, c_xz, c_yz = (0.5 * s for s in scaled[3:])
    c_0 = 1.0 - 2.0 * c_z
    split = parts // 2
    zero = jnp.zeros((ROWS, lanes), jnp.float32)

    def start(x, total):
        for j in range(split):
            for source, side in ((mine_ref, core), (other_ref, 1 - core)):
                at = side * split + j
                adjoint = source[x, j]
                half = half_ref[x, at]
                state = half * adjoint
                end = hist_ref[count, x, at]
                state_ref[0, x, at] = state
                square_ref[x, at] = half * half
                density_ref[x, at] = (-0.5 * end) * state
                total = total + end * adjoint
        return total

    partition = lax.fori_loop(0, planes, start, zero)
    trips, size = blocks(planes)

    def advance(step, sums):
        now, later = lax.rem(step, 2), lax.rem(step + 1, 2)

        def plane(x):
            x = lax.rem(x, planes)
            return [state_ref[now, x, j] for j in range(parts)]

        def block(trip, carry):
            minus, centre, sums = carry
            sums = list(sums)
            first = trip * size
            for i in range(size):
                x = first + i
                plus = plane(x + 1)
                diff = [p - m for p, m in zip(plus, minus)]
                total = [p + m for p, m in zip(plus, minus)]
                above, below = up_y(centre), down_y(centre)
                diff_above, diff_below = up_y(diff), down_y(diff)
                for j in range(parts):
                    paired = hist_ref[count - step, x, j]
                    twice = centre[j] + centre[j]
                    s_xx = total[j] - twice
                    s_yy = (above[j] + below[j]) - twice
                    d_xy = diff_above[j] - diff_below[j]
                    d_y = above[j] - below[j]
                    skew = c_xz * diff[j] + c_yz * d_y
                    main = c_z * centre[j]
                    value = (
                        c_0 * centre[j]
                        + c_x * s_xx
                        + c_y * s_yy
                        + c_xy * d_xy
                        + (up_z(main + skew) + down_z(main - skew))
                    )
                    state_ref[later, x, j] = square_ref[x, j] * value
                    paired_up, paired_down = up_z(paired), down_z(paired)
                    q_zz = (paired_up + paired_down) - (paired + paired)
                    q_z = paired_down - paired_up
                    density_ref[x, j] = density_ref[x, j] + paired * centre[j]
                    terms = (
                        paired * s_xx, paired * s_yy, q_zz * centre[j],
                        paired * d_xy, q_z * diff[j], q_z * d_y,
                    )
                    sums = [s + t for s, t in zip(sums, terms)]
                minus, centre = centre, plus
            return minus, centre, tuple(sums)

        return lax.fori_loop(0, trips, block, (plane(planes - 1), plane(0), sums))[2]

    sums = lax.fori_loop(0, count, advance, (zero,) * 6)
    last = lax.rem(count, 2)

    @pl.loop(0, planes)
    def _(x):
        for j in range(parts):
            final = 0.5 * (hist_ref[0, x, j] * state_ref[last, x, j])
            density = mu * (density_ref[x, j] + final) / half_ref[x, j]
            line_ref[x, pl.ds(j, ROWS, stride=parts), :] = density

    owners = out_ref.shape[0]
    cores = lax.axis_size("arm")
    depth, near = planes * cores // owners, line_ref.shape[1] // cores
    body = depth * near
    weights = (1.0, 1.0, 1.0, 0.25, 0.25, 0.25)
    for k in range(6):
        tail_ref[k : k + 1, :] = jnp.sum((weights[k] * mu) * sums[k], axis=0, keepdims=True)
    tail_ref[6:7, :] = jnp.sum(partition, axis=0, keepdims=True)
    tail_ref[7:8, :] = jnp.full((1, lanes), species_ref[arm].astype(jnp.float32), jnp.float32)

    @pl.loop(0, owners // cores)
    def _(slab):
        for side in range(cores):
            for i in range(depth):
                out_ref[slab * cores + side, i * near : (i + 1) * near, :] = line_ref[
                    slab * depth + i, side * near : (side + 1) * near, :
                ]
            out_ref[slab * cores + side, body : body + ROWS, :] = tail_ref[...]


def owner_kernel(arms, cores, cells, shares_ref, density_ref, stress_ref):
    species, depth, near, lanes = density_ref.shape
    body = depth * near
    senders = range(arms * cores)
    tails = [shares_ref[a, body : body + ROWS, :] for a in senders]
    total = tails[0]
    for a in senders[1:]:
        total = total + tails[a]
    partition = jnp.broadcast_to(jnp.sum(tails[0][6:7, :], axis=1, keepdims=True), (ROWS, lanes))
    norm = (arms * cores) * partition
    scale = cells / norm
    stress = total / norm
    for k in range(6):
        stress_ref[k] = jnp.sum(stress[k : k + 1, :])
    kinds = [jnp.broadcast_to(t[7:8, :], (ROWS, lanes)) for t in tails]
    for i in range(depth):
        for r in range(0, near, ROWS):
            values = [shares_ref[a, i * near + r : i * near + r + ROWS, :] for a in senders]
            for kind in range(species):
                picked = [jnp.where(kinds[a] == float(kind), values[a], 0.0) for a in senders]
                result = picked[0]
                for value in picked[1:]:
                    result = result + value
                density_ref[kind, i, r : r + ROWS, :] = result * scale


def local(field_w, metric, arm_length, arm_steps, arm_species):
    species, depth, rows, lanes = field_w.shape
    arms, slabs, cores = arm_length.shape[0], lax.axis_size("slab"), lax.axis_size("arm")
    assert slabs % arms == 0 and cores == 2 and rows % (2 * ROWS) == 0
    planes, parts = slabs * depth, rows // ROWS
    f32, vmem, smem = jnp.float32, pl.BlockSpec(memory_space=pltpu.VMEM), pl.BlockSpec(memory_space=pltpu.SMEM)
    params = pltpu.CompilerParams(vmem_limit_bytes=56 * 1024 * 1024)
    swap = [(0, 1), (1, 0)]

    wanted = jnp.tile(arm_species, slabs // arms)[:, None, None, None]
    chosen = jnp.broadcast_to(field_w[0][None], (slabs, depth, rows, lanes))
    for kind in range(1, species):
        chosen = jnp.where(wanted == kind, field_w[kind][None], chosen)
    field = lax.all_to_all(chosen, "slab", 0, 0, tiled=True)

    grid = (planes, parts, ROWS, lanes)
    piece = (planes, parts // 2, ROWS, lanes)
    hist, half, keep, give = pl.pallas_call(
        functools.partial(forward_kernel, arms),
        out_shape=[
            jax.ShapeDtypeStruct((STEPS + 1,) + grid, f32),
            jax.ShapeDtypeStruct(grid, f32),
            jax.ShapeDtypeStruct(piece, f32),
            jax.ShapeDtypeStruct(piece, f32),
        ],
        in_specs=[smem] * 3 + [vmem],
        out_specs=[vmem] * 4,
        compiler_params=params,
        name="forward",
    )(arm_length, arm_steps, metric, field)

    other = lax.ppermute(give, "arm", swap)
    flat = (slabs, depth * (parts // 2) * ROWS, lanes)
    pairs = lax.all_to_all((keep * other).reshape(flat), "slab", 0, 0, tiled=True)
    rest = pl.pallas_call(
        functools.partial(exclusive_kernel, arms),
        out_shape=jax.ShapeDtypeStruct(flat, f32),
        in_specs=[vmem],
        out_specs=vmem,
        name="exclusive",
    )(pairs)
    rest = lax.all_to_all(rest, "slab", 0, 0, tiled=True).reshape(piece)
    beyond = lax.ppermute(rest * keep, "arm", swap)

    body = depth * (rows // cores)
    shares = pl.pallas_call(
        functools.partial(adjoint_kernel, arms),
        out_shape=jax.ShapeDtypeStruct((slabs * cores, body + ROWS, lanes), f32),
        in_specs=[smem] * 4 + [vmem] * 4,
        out_specs=vmem,
        scratch_shapes=[
            pltpu.VMEM((2,) + grid, f32),
            pltpu.VMEM(grid, f32),
            pltpu.VMEM(grid, f32),
            pltpu.VMEM((planes, rows, lanes), f32),
            pltpu.VMEM((ROWS, lanes), f32),
        ],
        compiler_params=params,
        name="adjoint",
    )(arm_length, arm_steps, arm_species, metric, hist, half, rest * other, beyond)

    shares = lax.all_to_all(shares, ("slab", "arm"), 0, 0, tiled=True)
    cells = float(planes * rows * lanes)
    return pl.pallas_call(
        functools.partial(owner_kernel, arms, cores, cells),
        out_shape=[
            jax.ShapeDtypeStruct((species, depth, rows // cores, lanes), f32),
            jax.ShapeDtypeStruct((6,), f32),
        ],
        in_specs=[vmem],
        out_specs=[vmem, smem],
        name="owner",
    )(shares)


def solution(mesh):
    return jax.shard_map(
        local,
        mesh=mesh,
        in_specs=(P(None, ("phase", "slab"), None, None), P("phase"), P("arm"), P("arm"), P("arm")),
        out_specs=(P(None, ("phase", "slab"), "arm", None), P("phase")),
        check_vma=False,
    )
```

time: 644 us -> 178 us (0.28)
  other arithmetic: 291 us -> 3.46 us
  waiting for transfers between devices: 140 us -> 3.28 us
  Pallas kernels: 0 us -> 100 us
  local copies, waits for them, and re-layouts: 83.4 us -> 1.58 us
  starting transfers between devices: 73.3 us -> 0.01 us
  blocking collectives: 32 us -> 68.4 us
  between operations: 16.8 us -> 0.65 us
    ppermute x66 -> x2, waiting for transfers between devices: 140 us -> 3.28 us  [the longest x1 1.74 us: local(): other = lax.ppermute(give, 'arm', swap)]
    pallas_call x0 -> x4, Pallas kernels: none -> 100 us  [the longest x1 48.6 us: local(): pl.pallas_call(functools.partial(adjoint_kernel, arms), out_shape=jax.Sha...]
    dynamic_update_slice x16 -> x0, other arithmetic: 82.9 us -> none  [forward_block(): lax.dynamic_update_index_in_dim(history, extended, step_index + 1, 0)]
    slice x198 -> x0, local copies, waits for them, and re-layouts: 73.8 us -> none  [the longest x128 50.9 us: upward(): return jnp.roll(values, -1, along)]
    ppermute x66 -> x2, starting transfers between devices: 73.3 us -> 0.01 us  [the longest x1 0.01 us: local(): other = lax.ppermute(give, 'arm', swap)]
    reduce_sum x18 -> x0, other arithmetic: 69.9 us -> none  [the longest x16 67.8 us: backward_block(): jnp.sum(paired * second, axis=(1, 2, 3))]
    all_to_all x0 -> x4, blocking collectives: none -> 68.4 us  [the longest x1 21.7 us: local(): field = lax.all_to_all(chosen, 'slab', 0, 0, tiled=True)]
    select_n x20 -> x1, other arithmetic: 59.6 us -> 0.11 us  [local(): chosen = jnp.where(wanted == kind, field_w[kind][None], chosen)]
  transfers between devices with their start and end apart: 67 -> 2, of which waited for: 63 -> 2; matrix products, arithmetic and copies ran while one was open for 11% -> 0% of each run, Pallas kernels for 0% -> 0%
where the time goes in v1:
time: 178 us
  Pallas kernels  100 us (56%)
  blocking collectives  68.4 us (38%)
  other arithmetic  3.46 us (2%)
  waiting for transfers between devices  3.28 us (2%)
    pallas_call x1, Pallas kernels, local(): pl.pallas_call(functools.partial(adjoint_kernel, arms), out_shape=jax.Sha...  48.6 us
    pallas_call x1, Pallas kernels, local(): pl.pallas_call(functools.partial(forward_kernel, arms), out_shape=[jax.Sh...  48.1 us
    all_to_all x1, blocking collectives, local(): field = lax.all_to_all(chosen, 'slab', 0, 0, tiled=True)  21.7 us
    all_to_all x1, blocking collectives, local(): shares = lax.all_to_all(shares, ('slab', 'arm'), 0, 0, tiled=True)  21.5 us
    all_to_all x1, blocking collectives, local(): rest = lax.all_to_all(rest, 'slab', 0, 0, tiled=True).reshape(piece)  12.6 us
    all_to_all x1, blocking collectives, local(): lax.all_to_all((keep * other).reshape(flat), 'slab', 0, 0, tiled=True)  12.6 us
  transfers between devices with their start and end apart: 2, of which 2 were waited for; matrix products, arithmetic and copies ran while one was open for 0% of the time, Pallas kernels for 0%

profile of v1, /device:TPU:0, one launch (start us, length us, event | category | flops | bytes accessed | tf_op | source)
XLA Modules:
  0.0 177.6 jit_solution(1280100046480831545)
XLA Ops:
  0.6 0.7 broadcast_compare_fusion
  1.3 0.9 slice_bitcast_fusion.1
  2.2 0.1 broadcast_select_fusion
  2.3 21.7 %all_to_all.20.field_ref = f32[8,4,32,128]{3,2,1,0:T(8,128)} all-to-all(f32[8,4,32,128]{3,2,1,0:T(8,128)S(1)} %broadcast_select_fusion), channel_id=1, replica_groups=mesh['phase'=2,'slab'=8,'arm'=2] {'slab'}, dimensions={0} | all-to-all | bytes 1048576 | tf_op jit(solution)/shard_map/all_to_all | solution.py:277
  24.0 48.1 %forward.1 = (f32[17,32,4,8,128]{4,3,2,1,0:T(8,128)}, f32[32,4,8,128]{3,2,1,0:T(8,128)}, f32[32,2,8,128]{3,2,1,0:T(8,128)}, f32[32,2,8,128]{3,2,1,0:T(8,128)}) custom-call(f32[8]{0:T(128)} %length_ref.3, s32[8]{0:T(128)} %steps_ref.3, f32[6]{0:T(128)} %metric_ref.3, f32[8,4,32,128]{3,2,1,0:T(8,128)} %all_to_all.20.field_ref), custom_call_target="tpu_custom_call" | custom-call | tf_op jit(solution)/shard_map/forward/pallas_call | solution.py:281
  72.2 0.0 collective-permute-start
  72.2 1.7 collective-permute-done
  73.9 1.0 mul.9
  74.9 12.6 %all_to_all.21.pairs_ref = f32[8,64,128]{2,1,0:T(8,128)} all-to-all(f32[8,64,128]{2,1,0:T(8,128)S(1)} %bitcast.7), channel_id=1, replica_groups=mesh['phase'=2,'slab'=8,'arm'=2] {'slab'}, dimensions={0} | all-to-all | bytes 524288 | tf_op jit(solution)/shard_map/all_to_all | solution.py:297
  87.5 1.8 exclusive.1
  89.2 12.6 %all_to_all.22 = f32[8,64,128]{2,1,0:T(8,128)S(1)} all-to-all(f32[8,64,128]{2,1,0:T(8,128)} %exclusive.1), channel_id=1, replica_groups=mesh['phase'=2,'slab'=8,'arm'=2] {'slab'}, dimensions={0} | all-to-all | bytes 524288 | tf_op jit(solution)/shard_map/all_to_all | solution.py:305
  101.9 1.7 fusion
  103.6 0.0 collective-permute-start.1
  103.6 1.5 collective-permute-done.1.other_ref
  105.1 0.0 copy-start
  105.1 0.7 copy-done
  105.8 48.6 %adjoint.1 = f32[16,72,128]{2,1,0:T(8,128)} custom-call(f32[8]{0:T(128)} %length_ref.3, s32[8]{0:T(128)} %steps_ref.3, s32[8]{0:T(128)} %species_ref.1, f32[6]{0:T(128)} %metric_ref.3, f32[17,32,4,8,128]{4,3,2,1,0:T(8,128)} %get-tuple-element.6.hist_ref, f32[32,4,8,128]{3,2,1,0:T(8,128)} %get-tuple-element.7.half_ref, ...), custom_call_target="tpu_custom_call" | custom-call | tf_op jit(solution)/shard_map/adjoint/pallas_call | solution.py:309
  154.3 21.5 %all_to_all.23.shares_ref = f32[16,72,128]{2,1,0:T(8,128)} all-to-all(f32[16,72,128]{2,1,0:T(8,128)} %adjoint.1), channel_id=1, replica_groups=mesh['phase'=2,'slab'=8,'arm'=2] {'slab','arm'}, dimensions={0} | all-to-all | bytes 1179648 | tf_op jit(solution)/shard_map/all_to_all | solution.py:325
  175.8 1.8 %owner.1 = (f32[2,4,16,128]{3,2,1,0:T(8,128)}, f32[6]{0:T(128)}) custom-call(f32[16,72,128]{2,1,0:T(8,128)} %all_to_all.23.shares_ref), custom_call_target="tpu_custom_call" | custom-call | tf_op jit(solution)/shard_map/owner/pallas_call | solution.py:327
Async XLA Ops:
  72.2 1.7 collective-permute-start
  103.6 1.5 collective-permute-start.1
  105.1 0.7 copy-start

commit v2 on v1

v2 whole, which is shorter than its diff:
```python
import functools

import jax
import jax.numpy as jnp
from jax import lax
from jax.experimental import pallas as pl
from jax.experimental.pallas import tpu as pltpu
from jax.sharding import PartitionSpec as P

STEPS = 16
ROWS = 8


def up_y(parts):
    return parts[1:] + [pltpu.roll(parts[0], ROWS - 1, 0)]


def down_y(parts):
    return [pltpu.roll(parts[-1], 1, 0)] + parts[:-1]


def up_z(value):
    return pltpu.roll(value, value.shape[1] - 1, 1)


def down_z(value):
    return pltpu.roll(value, 1, 1)


def splat(scalar, lanes):
    return jnp.full((ROWS, lanes), scalar, jnp.float32)


def coefficients(arm, lanes, length_ref, steps_ref, metric_ref):
    mu = splat(length_ref[arm], lanes) / splat(steps_ref[arm].astype(jnp.float32), lanes)
    return mu, [mu * metric_ref[k] for k in range(3)] + [(0.5 * mu) * metric_ref[k] for k in range(3, 6)]


def put(state, x, j, value):
    value_ref, sum_ref, slope_ref = state
    above, below = up_z(value), down_z(value)
    value_ref[x, j] = value
    sum_ref[x, j] = above + below
    slope_ref[x, j] = above - below


def sweep(state, visit):
    value_ref, sum_ref, slope_ref = state
    planes, parts = value_ref.shape[:2]

    def plane(ref, x):
        return [ref[x % planes, j] for j in range(parts)]

    minus, centre = plane(value_ref, -1), plane(value_ref, 0)
    slope_minus, slope = plane(slope_ref, -1), plane(slope_ref, 0)
    for x in range(planes):
        plus, slope_plus = plane(value_ref, x + 1), plane(slope_ref, x + 1)
        diff = [p - m for p, m in zip(plus, minus)]
        above, below = up_y(centre), down_y(centre)
        for j in range(parts):
            visit(
                x, j, centre[j], plus[j] + minus[j], above[j] + below[j], sum_ref[x, j], diff,
                slope_plus[j] - slope_minus[j], slope,
            )
        minus, centre = centre, plus
        slope_minus, slope = slope, slope_plus


def in_pairs(count, step, first, second, carry):
    def both(k, carry):
        carry = step(2 * k, first, second, carry)
        return lax.cond(
            2 * k + 1 < count, lambda c: step(2 * k + 1, second, first, c), lambda c: c, carry
        )

    return lax.fori_loop(0, (count + 1) // 2, both, carry)


def forward_kernel(
    arms, length_ref, steps_ref, metric_ref, field_ref, hist_ref, half_ref, keep_ref, give_ref, *scratch
):
    _, planes, parts, _, lanes = hist_ref.shape
    slabs, depth = field_ref.shape[:2]
    arm, core = lax.rem(lax.axis_index("slab"), arms), lax.axis_index("arm")
    count = steps_ref[arm]
    mu, (c_x, c_y, c_z, c_xy, c_xz, c_yz) = coefficients(arm, lanes, length_ref, steps_ref, metric_ref)
    c_0 = 1.0 - 2.0 * (c_x + c_y + c_z)
    decay = -0.5 * mu
    first, second = scratch[:3], scratch[3:]

    for x in range(planes):
        for j in range(parts):
            half = jnp.exp(decay * field_ref[x // depth, x % depth, pl.ds(j, ROWS, stride=parts), :])
            half_ref[x, j] = half
            put(first, x, j, half)

    def step(k, source, target, carry):
        def visit(x, j, centre, sum_x, sum_y, sum_z, diff, slope_x, slope):
            if j == 0:
                skew = [c_xy * d + c_yz * s for d, s in zip(diff, slope)]
                visit.skew = [a - b for a, b in zip(up_y(skew), down_y(skew))]
            value = (
                (c_0 * centre + c_x * sum_x) + (c_y * sum_y + c_z * sum_z) + (c_xz * slope_x + visit.skew[j])
            )
            half = half_ref[x, j]
            value = half * value
            hist_ref[k, x, j] = value
            put(target, x, j, half * value)

        sweep(source, visit)
        return carry

    in_pairs(count, step, first, second, 0)
    split = parts // 2
    for x in range(planes):
        for j in range(split):
            keep_ref[x, j] = hist_ref[count - 1, x, core * split + j]
            give_ref[x, j] = hist_ref[count - 1, x, (1 - core) * split + j]


def exclusive_kernel(arms, pairs_ref, out_ref):
    slabs, rows, _ = pairs_ref.shape

    @pl.loop(0, rows // ROWS)
    def _(block):
        at = pl.ds(pl.multiple_of(block * ROWS, ROWS), ROWS)
        values = [pairs_ref[a, at, :] for a in range(arms)]
        before, after = [None] * arms, [None] * arms
        for a in range(1, arms):
            before[a] = values[a - 1] if before[a - 1] is None else before[a - 1] * values[a - 1]
            b = arms - 1 - a
            after[b] = values[b + 1] if after[b + 1] is None else after[b + 1] * values[b + 1]
        for a in range(arms):
            sides = [s for s in (before[a], after[a]) if s is not None]
            result = sides[0] * sides[1] if len(sides) == 2 else sides[0]
            for copy in range(a, slabs, arms):
                out_ref[copy, at, :] = result


def adjoint_kernel(
    arms, length_ref, steps_ref, species_ref, metric_ref, hist_ref, half_ref, mine_ref, other_ref, out_ref,
    square_ref, density_ref, line_ref, tail_ref, *scratch,
):
    _, planes, parts, _, lanes = hist_ref.shape
    arm, core = lax.rem(lax.axis_index("slab"), arms), lax.axis_index("arm")
    count = steps_ref[arm]
    mu, (c_x, c_y, c_z, c_xy, c_xz, c_yz) = coefficients(arm, lanes, length_ref, steps_ref, metric_ref)
    first, second = scratch[:3], scratch[3:]
    split = parts // 2
    zero = jnp.zeros((ROWS, lanes), jnp.float32)

    partition = zero
    for x in range(planes):
        for j in range(split):
            for source, side in ((mine_ref, core), (other_ref, 1 - core)):
                at = side * split + j
                adjoint = source[x, j]
                half = half_ref[x, at]
                value = half * adjoint
                end = hist_ref[count - 1, x, at]
                put(first, x, at, value)
                square_ref[x, at] = half * half
                density_ref[x, at] = (-0.5 * end) * value
                partition = partition + end * adjoint

    def step(k, source, target, sums):
        sums = list(sums)

        def visit(x, j, centre, sum_x, sum_y, sum_z, diff, slope_x, slope):
            if j == 0:
                visit.d_xy = [a - b for a, b in zip(up_y(diff), down_y(diff))]
                visit.d_yz = [a - b for a, b in zip(up_y(slope), down_y(slope))]
            twice = centre + centre
            s_xx, s_yy, s_zz = sum_x - twice, sum_y - twice, sum_z - twice
            s_xy, s_yz = visit.d_xy[j], visit.d_yz[j]
            value = (
                (centre + c_x * s_xx) + (c_y * s_yy + c_z * s_zz)
                + (c_xz * slope_x + (c_xy * s_xy + c_yz * s_yz))
            )
            put(target, x, j, square_ref[x, j] * value)
            paired = hist_ref[count - 1 - k, x, j]
            density_ref[x, j] = density_ref[x, j] + paired * centre
            for i, term in enumerate((s_xx, s_yy, s_zz, s_xy, slope_x, s_yz)):
                sums[i] = sums[i] + paired * term

        sweep(source, visit)
        return tuple(sums)

    sums = in_pairs(count, step, first, second, (zero,) * 6)

    def finish(value_ref):
        for x in range(planes):
            for j in range(parts):
                density = density_ref[x, j] + 0.5 * value_ref[x, j]
                line_ref[x, pl.ds(j, ROWS, stride=parts), :] = mu * density / half_ref[x, j]

    even = lax.rem(count, 2) == 0
    pl.when(even)(lambda: finish(first[0]))
    pl.when(jnp.logical_not(even))(lambda: finish(second[0]))

    owners = out_ref.shape[0]
    cores = lax.axis_size("arm")
    depth, near = planes * cores // owners, line_ref.shape[1] // cores
    body = depth * near
    weights = (1.0, 1.0, 1.0, 0.25, 0.25, 0.25)
    for k in range(6):
        tail_ref[k : k + 1, :] = jnp.sum((weights[k] * mu) * sums[k], axis=0, keepdims=True)
    tail_ref[6:7, :] = jnp.sum(partition, axis=0, keepdims=True)
    tail_ref[7:8, :] = jnp.full((1, lanes), species_ref[arm].astype(jnp.float32), jnp.float32)

    @pl.loop(0, owners // cores)
    def _(slab):
        for side in range(cores):
            for i in range(depth):
                out_ref[slab * cores + side, i * near : (i + 1) * near, :] = line_ref[
                    slab * depth + i, side * near : (side + 1) * near, :
                ]
            out_ref[slab * cores + side, body : body + ROWS, :] = tail_ref[...]


def owner_kernel(arms, cores, cells, shares_ref, density_ref, stress_ref):
    species, depth, near, lanes = density_ref.shape
    body = depth * near
    senders = range(arms * cores)
    tails = [shares_ref[a, body : body + ROWS, :] for a in senders]
    total = tails[0]
    for a in senders[1:]:
        total = total + tails[a]
    partition = jnp.broadcast_to(jnp.sum(tails[0][6:7, :], axis=1, keepdims=True), (ROWS, lanes))
    norm = (arms * cores) * partition
    scale = cells / norm
    stress = total / norm
    for k in range(6):
        stress_ref[k] = jnp.sum(stress[k : k + 1, :])
    kinds = [jnp.broadcast_to(t[7:8, :], (ROWS, lanes)) for t in tails]
    for i in range(depth):
        for r in range(0, near, ROWS):
            values = [shares_ref[a, i * near + r : i * near + r + ROWS, :] for a in senders]
            for kind in range(species):
                picked = [jnp.where(kinds[a] == float(kind), values[a], 0.0) for a in senders]
                result = picked[0]
                for value in picked[1:]:
                    result = result + value
                density_ref[kind, i, r : r + ROWS, :] = result * scale


def local(field_w, metric, arm_length, arm_steps, arm_species):
    species, depth, rows, lanes = field_w.shape
    arms, slabs, cores = arm_length.shape[0], lax.axis_size("slab"), lax.axis_size("arm")
    assert slabs % arms == 0 and cores == 2 and rows % (2 * ROWS) == 0
    planes, parts = slabs * depth, rows // ROWS
    f32, vmem, smem = jnp.float32, pl.BlockSpec(memory_space=pltpu.VMEM), pl.BlockSpec(memory_space=pltpu.SMEM)
    size = 4 * planes * rows * lanes
    params = pltpu.CompilerParams(vmem_limit_bytes=(STEPS + 16) * size)
    small = pltpu.CompilerParams(vmem_limit_bytes=8 * size)
    swap = [(0, 1), (1, 0)]

    wanted = jnp.tile(arm_species, slabs // arms)[:, None, None, None]
    chosen = jnp.broadcast_to(field_w[0][None], (slabs, depth, rows, lanes))
    for kind in range(1, species):
        chosen = jnp.where(wanted == kind, field_w[kind][None], chosen)
    field = lax.all_to_all(chosen, "slab", 0, 0, tiled=True)

    grid = (planes, parts, ROWS, lanes)
    piece = (planes, parts // 2, ROWS, lanes)
    hist, half, keep, give = pl.pallas_call(
        functools.partial(forward_kernel, arms),
        out_shape=[
            jax.ShapeDtypeStruct((STEPS,) + grid, f32),
            jax.ShapeDtypeStruct(grid, f32),
            jax.ShapeDtypeStruct(piece, f32),
            jax.ShapeDtypeStruct(piece, f32),
        ],
        in_specs=[smem] * 3 + [vmem],
        out_specs=[vmem] * 4,
        scratch_shapes=[pltpu.VMEM(grid, f32)] * 6,
        compiler_params=params,
        name="forward",
    )(arm_length, arm_steps, metric, field)

    other = lax.ppermute(give, "arm", swap)
    flat = (slabs, depth * (parts // 2) * ROWS, lanes)
    pairs = lax.all_to_all((keep * other).reshape(flat), "slab", 0, 0, tiled=True)
    rest = pl.pallas_call(
        functools.partial(exclusive_kernel, arms),
        out_shape=jax.ShapeDtypeStruct(flat, f32),
        in_specs=[vmem],
        out_specs=vmem,
        compiler_params=small,
        name="exclusive",
    )(pairs)
    rest = lax.all_to_all(rest, "slab", 0, 0, tiled=True).reshape(piece)
    beyond = lax.ppermute(rest * keep, "arm", swap)

    body = depth * (rows // cores)
    shares = pl.pallas_call(
        functools.partial(adjoint_kernel, arms),
        out_shape=jax.ShapeDtypeStruct((slabs * cores, body + ROWS, lanes), f32),
        in_specs=[smem] * 4 + [vmem] * 4,
        out_specs=vmem,
        scratch_shapes=[
            pltpu.VMEM(grid, f32),
            pltpu.VMEM(grid, f32),
            pltpu.VMEM((planes, rows, lanes), f32),
            pltpu.VMEM((ROWS, lanes), f32),
        ]
        + [pltpu.VMEM(grid, f32)] * 6,
        compiler_params=params,
        name="adjoint",
    )(arm_length, arm_steps, arm_species, metric, hist, half, rest * other, beyond)

    shares = lax.all_to_all(shares, ("slab", "arm"), 0, 0, tiled=True)
    cells = float(planes * rows * lanes)
    return pl.pallas_call(
        functools.partial(owner_kernel, arms, cores, cells),
        out_shape=[
            jax.ShapeDtypeStruct((species, depth, rows // cores, lanes), f32),
            jax.ShapeDtypeStruct((6,), f32),
        ],
        in_specs=[vmem],
        out_specs=[vmem, smem],
        compiler_params=small,
        name="owner",
    )(shares)


def solution(mesh):
    return jax.shard_map(
        local,
        mesh=mesh,
        in_specs=(P(None, ("phase", "slab"), None, None), P("phase"), P("arm"), P("arm"), P("arm")),
        out_specs=(P(None, ("phase", "slab"), "arm", None), P("phase")),
        check_vma=False,
    )
```

time: 178 us -> 97.5 us (0.55)
  Pallas kernels: 100 us -> 14.5 us
  blocking collectives: 68.4 us -> 74.6 us
  other arithmetic: 3.46 us -> 0.85 us
  local copies, waits for them, and re-layouts: 1.58 us -> 3.5 us
    pallas_call x1, Pallas kernels: 48.1 us -> 5.39 us  [local(): pl.pallas_call(functools.partial(forward_kernel, arms), out_shape=[jax.Sh...]
    pallas_call x1, Pallas kernels: 48.6 us -> 8.26 us  [local(): pl.pallas_call(functools.partial(adjoint_kernel, arms), out_shape=jax.Sha...]
    all_to_all x1, blocking collectives: 21.5 us -> 25.5 us  [local(): shares = lax.all_to_all(shares, ('slab', 'arm'), 0, 0, tiled=True)]
    all_to_all x1, blocking collectives: 12.6 us -> 15.6 us  [local(): lax.all_to_all((keep * other).reshape(flat), 'slab', 0, 0, tiled=True)]
    unnamed x2 -> x8, local copies, waits for them, and re-layouts: 0.7 us -> 2.62 us
where the time goes in v2:
time: 97.5 us; the launch traced here: 97.3 us
  blocking collectives  74.6 us (77%)
  Pallas kernels  14.5 us (15%)
  local copies, waits for them, and re-layouts  3.5 us (4%)
  waiting for transfers between devices  3.04 us (3%)
    all_to_all x1, blocking collectives, local(): shares = lax.all_to_all(shares, ('slab', 'arm'), 0, 0, tiled=True)  25.5 us
    all_to_all x1, blocking collectives, local(): field = lax.all_to_all(chosen, 'slab', 0, 0, tiled=True)  21.6 us
    all_to_all x1, blocking collectives, local(): lax.all_to_all((keep * other).reshape(flat), 'slab', 0, 0, tiled=True)  15.6 us
    all_to_all x1, blocking collectives, local(): rest = lax.all_to_all(rest, 'slab', 0, 0, tiled=True).reshape(piece)  12 us
    pallas_call x1, Pallas kernels, local(): pl.pallas_call(functools.partial(adjoint_kernel, arms), out_shape=jax.Sha...  8.26 us
    pallas_call x1, Pallas kernels, local(): pl.pallas_call(functools.partial(forward_kernel, arms), out_shape=[jax.Sh...  5.39 us
    unnamed x8, local copies, waits for them, and re-layouts  2.62 us
  transfers between devices with their start and end apart: 2, of which 2 were waited for; matrix products, arithmetic and copies ran while one was open for 0% of the time, Pallas kernels for 0%

profile of v2, /device:TPU:0, one launch (start us, length us, event | category | flops | bytes accessed | tf_op | source)
XLA Modules:
  0.0 97.3 jit_solution(9418664744781055997)
XLA Ops:
  0.6 0.7 broadcast_compare_fusion
  1.3 0.9 slice_bitcast_fusion.1
  2.2 0.1 broadcast_select_fusion
  2.3 21.6 %all_to_all.20.field_ref = f32[8,4,32,128]{3,2,1,0:T(8,128)S(1)} all-to-all(f32[8,4,32,128]{3,2,1,0:T(8,128)S(1)} %broadcast_select_fusion), channel_id=1, replica_groups=mesh['phase'=2,'slab'=8,'arm'=2] {'slab'}, dimensions={0} | all-to-all | bytes 1048576 | tf_op jit(solution)/shard_map/all_to_all | solution.py:262
  23.9 0.0 copy-start
  23.9 0.7 copy-done
  24.6 0.0 copy-start.1
  24.6 0.7 copy-done.1
  25.2 0.0 copy-start.2
  25.2 0.7 copy-done.2
  25.9 5.4 %forward.1 = (f32[16,32,4,8,128]{4,3,2,1,0:T(8,128)S(1)}, f32[32,4,8,128]{3,2,1,0:T(8,128)S(1)}, f32[32,2,8,128]{3,2,1,0:T(8,128)S(1)}, f32[32,2,8,128]{3,2,1,0:T(8,128)S(1)}) custom-call(f32[8]{0:T(128)S(1)} %copy-done, s32[8]{0:T(128)S(1)} %copy-done.1, f32[6]{0:T(128)S(1)} %copy-done.2, f32[8,4,32,128]{3,2,1,0:T(8,128)S(1)} %all_to_all.20.field_ref), custom_call_target="tpu_custom_call" | custom-call | tf_op jit(solution)/shard_map/forward/pallas_call | solution.py:266
  31.3 0.1 collective-permute-start
  31.4 1.5 %collective-permute-done = f32[32,2,8,128]{3,2,1,0:T(8,128)S(1)} collective-permute-done((f32[32,2,8,128]{3,2,1,0:T(8,128)S(1)}, f32[32,2,8,128]{3,2,1,0:T(8,128)S(1)}, u32[]{:S(2)}, u32[]{:S(2)}) %collective-permute-start) | collective-permute-done | bytes 262176 | tf_op jit(solution)/shard_map/ppermute | solution.py:281
  32.9 15.6 %all_to_all.21.pairs_ref = f32[8,64,128]{2,1,0:T(8,128)S(1)} all-to-all(f32[8,64,128]{2,1,0:T(8,128)S(1)} %bitcast.7), channel_id=1, replica_groups=mesh['phase'=2,'slab'=8,'arm'=2] {'slab'}, dimensions={0} | all-to-all | bytes 524288 | tf_op jit(solution)/shard_map/all_to_all | solution.py:283
  48.5 0.1 exclusive.1
  48.6 12.0 %all_to_all.22 = f32[8,64,128]{2,1,0:T(8,128)S(1)} all-to-all(f32[8,64,128]{2,1,0:T(8,128)S(1)} %exclusive.1), channel_id=1, replica_groups=mesh['phase'=2,'slab'=8,'arm'=2] {'slab'}, dimensions={0} | all-to-all | bytes 524288 | tf_op jit(solution)/shard_map/all_to_all | solution.py:292
  60.5 0.1 fusion
  60.6 0.1 collective-permute-start.1
  60.7 1.5 %collective-permute-done.1.other_ref = f32[32,2,8,128]{3,2,1,0:T(8,128)S(1)} collective-permute-done((f32[32,2,8,128]{3,2,1,0:T(8,128)S(1)}, f32[32,2,8,128]{3,2,1,0:T(8,128)S(1)}, u32[]{:S(2)}, u32[]{:S(2)}) %collective-permute-start.1) | collective-permute-done | bytes 262176 | tf_op jit(solution)/shard_map/ppermute | solution.py:293
  62.2 0.0 copy-start.3
  62.2 0.7 copy-done.3
  62.8 8.3 %adjoint.1 = f32[16,72,128]{2,1,0:T(8,128)S(1)} custom-call(f32[8]{0:T(128)S(1)} %copy-done, s32[8]{0:T(128)S(1)} %copy-done.1, s32[8]{0:T(128)S(1)} %copy-done.3, f32[6]{0:T(128)S(1)} %copy-done.2, f32[16,32,4,8,128]{4,3,2,1,0:T(8,128)S(1)} %get-tuple-element.6.hist_ref, f32[32,4,8,128]{3,2,1,0:T(8,128)S(1)} %get-tuple-element.7.half_ref, ...), custom_call_target="tpu_custom_call" | custom-call | tf_op jit(solution)/shard_map/adjoint/pallas_call | solution.py:296
  71.1 25.5 %all_to_all.23.shares_ref = f32[16,72,128]{2,1,0:T(8,128)S(1)} all-to-all(f32[16,72,128]{2,1,0:T(8,128)S(1)} %adjoint.1), channel_id=1, replica_groups=mesh['phase'=2,'slab'=8,'arm'=2] {'slab','arm'}, dimensions={0} | all-to-all | bytes 1179648 | tf_op jit(solution)/shard_map/all_to_all | solution.py:312
  96.6 0.7 owner.1
  (1 shorter events, 0.0 us)
Async XLA Ops:
  23.9 0.7 copy-start
  24.6 0.7 copy-start.1
  25.2 0.7 copy-start.2
  31.3 1.6 %collective-permute-start = (f32[32,2,8,128]{3,2,1,0:T(8,128)S(1)}, f32[32,2,8,128]{3,2,1,0:T(8,128)S(1)}, u32[]{:S(2)}, u32[]{:S(2)}) collective-permute-start(f32[32,2,8,128]{3,2,1,0:T(8,128)S(1)} %get-tuple-element.9), channel_id=1, source_target_pairs={{0,1},{1,0},{2,3},{3,2},{4,5},{5,4},{6,7},{7,6},{8,9},{9,8},{10,11... | collective-permute-start | bytes 786440 | tf_op jit(solution)/shard_map/ppermute | solution.py:281
  60.6 1.6 %collective-permute-start.1 = (f32[32,2,8,128]{3,2,1,0:T(8,128)S(1)}, f32[32,2,8,128]{3,2,1,0:T(8,128)S(1)}, u32[]{:S(2)}, u32[]{:S(2)}) collective-permute-start(f32[32,2,8,128]{3,2,1,0:T(8,128)S(1)} %get-tuple-element.10), channel_id=1, source_target_pairs={{0,1},{1,0},{2,3},{3,2},{4,5},{5,4},{6,7},{7,6},{8,9},{9,8},{10,11... | collective-permute-start | bytes 786440 | tf_op jit(solution)/shard_map/ppermute | solution.py:293
  62.2 0.7 copy-start.3

commit v3 on v2

--- a/solution.py
+++ b/solution.py
@@ -31,9 +31,33 @@
     return jnp.full((ROWS, lanes), scalar, jnp.float32)
 
 
-def coefficients(arm, lanes, length_ref, steps_ref, metric_ref):
-    mu = splat(length_ref[arm], lanes) / splat(steps_ref[arm].astype(jnp.float32), lanes)
-    return mu, [mu * metric_ref[k] for k in range(3)] + [(0.5 * mu) * metric_ref[k] for k in range(3, 6)]
+MU, COUNT, SPECIES, METRIC = 0, 1, 2, 3
+
+
+def prepare_kernel(*refs):
+    sources, (chosen_ref, table_ref), targets, sems = refs[:5], refs[5:7], refs[7:12], refs[12]
+    copies = [pltpu.make_async_copy(s, t, sems.at[i]) for i, (s, t) in enumerate(zip(sources, targets))]
+    for copy in copies:
+        copy.start()
+    for copy in copies:
+        copy.wait()
+    length_ref, steps_ref, species_ref, metric_ref, field_ref = targets
+    arms, (slabs, lanes) = length_ref.shape[0], (chosen_ref.shape[0], table_ref.shape[2])
+    arm = lax.rem(lax.axis_index("slab"), arms)
+    steps = splat(steps_ref[arm].astype(jnp.float32), lanes)
+    mu = splat(length_ref[arm], lanes) / steps
+    table_ref[MU] = mu
+    table_ref[COUNT] = steps
+    table_ref[SPECIES] = splat(species_ref[arm].astype(jnp.float32), lanes)
+    for k in range(6):
+        table_ref[METRIC + k] = (mu if k < 3 else 0.5 * mu) * metric_ref[k]
+    for slab in range(slabs):
+        chosen_ref[slab] = field_ref[species_ref[slab % arms]]
+
+
+def unpack(table_ref):
+    count = table_ref[COUNT][0, 0].astype(jnp.int32)
+    return count, table_ref[MU], [table_ref[METRIC + k] for k in range(6)]
 
 
 def put(state, x, j, value):
@@ -76,15 +100,13 @@
     return lax.fori_loop(0, (count + 1) // 2, both, carry)
 
 
-def forward_kernel(
-    arms, length_ref, steps_ref, metric_ref, field_ref, hist_ref, half_ref, keep_ref, give_ref, *scratch
-):
-    _, planes, parts, _, lanes = hist_ref.shape
-    slabs, depth = field_ref.shape[:2]
-    arm, core = lax.rem(lax.axis_index("slab"), arms), lax.axis_index("arm")
-    count = steps_ref[arm]
-    mu, (c_x, c_y, c_z, c_xy, c_xz, c_yz) = coefficients(arm, lanes, length_ref, steps_ref, metric_ref)
+def forward_kernel(table_ref, field_ref, hist_ref, half_ref, keep_ref, give_ref, gain_ref, *scratch):
+    planes, parts = half_ref.shape[:2]
+    depth = field_ref.shape[1]
+    core = lax.axis_index("arm")
+    count, mu, (c_x, c_y, c_z, c_xy, c_xz, c_yz) = unpack(table_ref)
     c_0 = 1.0 - 2.0 * (c_x + c_y + c_z)
+    c_0, c_y, c_z, c_xy, c_xz, c_yz = (c / c_x for c in (c_0, c_y, c_z, c_xy, c_xz, c_yz))
     decay = -0.5 * mu
     first, second = scratch[:3], scratch[3:]
 
@@ -92,6 +114,7 @@
         for j in range(parts):
             half = jnp.exp(decay * field_ref[x // depth, x % depth, pl.ds(j, ROWS, stride=parts), :])
             half_ref[x, j] = half
+            gain_ref[x, j] = c_x * half
             put(first, x, j, half)
 
     def step(k, source, target, carry):
@@ -100,12 +123,11 @@
                 skew = [c_xy * d + c_yz * s for d, s in zip(diff, slope)]
                 visit.skew = [a - b for a, b in zip(up_y(skew), down_y(skew))]
             value = (
-                (c_0 * centre + c_x * sum_x) + (c_y * sum_y + c_z * sum_z) + (c_xz * slope_x + visit.skew[j])
+                (c_0 * centre + sum_x) + (c_y * sum_y + c_z * sum_z) + (c_xz * slope_x + visit.skew[j])
             )
-            half = half_ref[x, j]
-            value = half * value
+            value = gain_ref[x, j] * value
             hist_ref[k, x, j] = value
-            put(target, x, j, half * value)
+            put(target, x, j, half_ref[x, j] * value)
 
         sweep(source, visit)
         return carry
@@ -138,13 +160,11 @@
 
 
 def adjoint_kernel(
-    arms, length_ref, steps_ref, species_ref, metric_ref, hist_ref, half_ref, mine_ref, other_ref, out_ref,
-    square_ref, density_ref, line_ref, tail_ref, *scratch,
+    table_ref, hist_ref, half_ref, mine_ref, other_ref, out_ref, square_ref, density_ref, line_ref, tail_ref, *scratch
 ):
-    _, planes, parts, _, lanes = hist_ref.shape
-    arm, core = lax.rem(lax.axis_index("slab"), arms), lax.axis_index("arm")
-    count = steps_ref[arm]
-    mu, (c_x, c_y, c_z, c_xy, c_xz, c_yz) = coefficients(arm, lanes, length_ref, steps_ref, metric_ref)
+    planes, parts, _, lanes = half_ref.shape
+    core = lax.axis_index("arm")
+    count, mu, (c_x, c_y, c_z, c_xy, c_xz, c_yz) = unpack(table_ref)
     first, second = scratch[:3], scratch[3:]
     split = parts // 2
     zero = jnp.zeros((ROWS, lanes), jnp.float32)
@@ -206,7 +226,7 @@
     for k in range(6):
         tail_ref[k : k + 1, :] = jnp.sum((weights[k] * mu) * sums[k], axis=0, keepdims=True)
     tail_ref[6:7, :] = jnp.sum(partition, axis=0, keepdims=True)
-    tail_ref[7:8, :] = jnp.full((1, lanes), species_ref[arm].astype(jnp.float32), jnp.float32)
+    tail_ref[7:8, :] = table_ref[SPECIES, 0:1, :]
 
     @pl.loop(0, owners // cores)
     def _(slab):
@@ -255,28 +275,38 @@
     small = pltpu.CompilerParams(vmem_limit_bytes=8 * size)
     swap = [(0, 1), (1, 0)]
 
-    wanted = jnp.tile(arm_species, slabs // arms)[:, None, None, None]
-    chosen = jnp.broadcast_to(field_w[0][None], (slabs, depth, rows, lanes))
-    for kind in range(1, species):
-        chosen = jnp.where(wanted == kind, field_w[kind][None], chosen)
+    arguments = (arm_length, arm_steps, arm_species, metric, field_w)
+    chosen, table = pl.pallas_call(
+        prepare_kernel,
+        out_shape=[
+            jax.ShapeDtypeStruct((slabs, depth, rows, lanes), f32),
+            jax.ShapeDtypeStruct((METRIC + 6, ROWS, lanes), f32),
+        ],
+        in_specs=[pl.BlockSpec(memory_space=pltpu.HBM)] * 5,
+        out_specs=[vmem] * 2,
+        scratch_shapes=[pltpu.SMEM(a.shape, a.dtype) for a in arguments[:4]]
+        + [pltpu.VMEM(field_w.shape, f32), pltpu.SemaphoreType.DMA((5,))],
+        compiler_params=small,
+        name="prepare",
+    )(*(pltpu.with_memory_space_constraint(a, pltpu.HBM) for a in arguments))
     field = lax.all_to_all(chosen, "slab", 0, 0, tiled=True)
 
     grid = (planes, parts, ROWS, lanes)
     piece = (planes, parts // 2, ROWS, lanes)
     hist, half, keep, give = pl.pallas_call(
-        functools.partial(forward_kernel, arms),
+        forward_kernel,
         out_shape=[
             jax.ShapeDtypeStruct((STEPS,) + grid, f32),
             jax.ShapeDtypeStruct(grid, f32),
             jax.ShapeDtypeStruct(piece, f32),
             jax.ShapeDtypeStruct(piece, f32),
         ],
-        in_specs=[smem] * 3 + [vmem],
+        in_specs=[vmem] * 2,
         out_specs=[vmem] * 4,
-        scratch_shapes=[pltpu.VMEM(grid, f32)] * 6,
+        scratch_shapes=[pltpu.VMEM(grid, f32)] * 7,
         compiler_params=params,
         name="forward",
-    )(arm_length, arm_steps, metric, field)
+    )(table, field)
 
     other = lax.ppermute(give, "arm", swap)
     flat = (slabs, depth * (parts // 2) * ROWS, lanes)
@@ -294,9 +324,9 @@
 
     body = depth * (rows // cores)
     shares = pl.pallas_call(
-        functools.partial(adjoint_kernel, arms),
+        adjoint_kernel,
         out_shape=jax.ShapeDtypeStruct((slabs * cores, body + ROWS, lanes), f32),
-        in_specs=[smem] * 4 + [vmem] * 4,
+        in_specs=[vmem] * 5,
         out_specs=vmem,
         scratch_shapes=[
             pltpu.VMEM(grid, f32),
@@ -307,7 +337,7 @@
         + [pltpu.VMEM(grid, f32)] * 6,
         compiler_params=params,
         name="adjoint",
-    )(arm_length, arm_steps, arm_species, metric, hist, half, rest * other, beyond)
+    )(table, hist, half, rest * other, beyond)
 
     shares = lax.all_to_all(shares, ("slab", "arm"), 0, 0, tiled=True)
     cells = float(planes * rows * lanes)

time: 97.5 us -> 92.4 us (0.948)
  local copies, waits for them, and re-layouts: 3.5 us -> 0 us
    unnamed x8 -> x0, local copies, waits for them, and re-layouts: 2.62 us -> none
    pallas_call x2 -> x3, Pallas kernels: 13.6 us -> 13.5 us  [the longest x1 7.88 us: local(): pl.pallas_call(adjoint_kernel, out_shape=jax.ShapeDtypeStruct((slabs * co...]
where the time goes in v3:
time: 92.4 us
  blocking collectives  74.2 us (80%)
  Pallas kernels  14.3 us (15%)
  waiting for transfers between devices  3.04 us (3%)
    all_to_all x1, blocking collectives, local(): shares = lax.all_to_all(shares, ('slab', 'arm'), 0, 0, tiled=True)  25.6 us
    all_to_all x1, blocking collectives, local(): field = lax.all_to_all(chosen, 'slab', 0, 0, tiled=True)  21.6 us
    all_to_all x1, blocking collectives, local(): lax.all_to_all((keep * other).reshape(flat), 'slab', 0, 0, tiled=True)  15 us
    all_to_all x1, blocking collectives, local(): rest = lax.all_to_all(rest, 'slab', 0, 0, tiled=True).reshape(piece)  12 us
    pallas_call x1, Pallas kernels, local(): pl.pallas_call(adjoint_kernel, out_shape=jax.ShapeDtypeStruct((slabs * co...  7.88 us
    pallas_call x1, Pallas kernels, local(): pl.pallas_call(forward_kernel, out_shape=[jax.ShapeDtypeStruct((STEPS,) +...  4.6 us
  transfers between devices with their start and end apart: 2, of which 2 were waited for; matrix products, arithmetic and copies ran while one was open for 0% of the time, Pallas kernels for 0%

profile of v3, /device:TPU:0, one launch (start us, length us, event | category | flops | bytes accessed | tf_op | source)
XLA Modules:
  0.0 92.4 jit_solution(14063419756884084891)
XLA Ops:
  0.6 1.0 %prepare.1 = (f32[8,4,32,128]{3,2,1,0:T(8,128)S(1)}, f32[9,8,128]{2,1,0:T(8,128)S(1)}) custom-call(f32[8]{0:T(128)} %refs_0_.1, s32[8]{0:T(128)} %refs_1_.1, s32[8]{0:T(128)} %refs_2_.1, f32[6]{0:T(128)} %refs_3_.1, f32[2,4,32,128]{3,2,1,0:T(8,128)} %refs_4_.1), custom_call_target="tpu_custom_call" | custom-call | tf_op jit(solution)/shard_map/prepare/pallas_call | solution.py:279
  1.6 21.6 %all_to_all.20.field_ref = f32[8,4,32,128]{3,2,1,0:T(8,128)S(1)} all-to-all(f32[8,4,32,128]{3,2,1,0:T(8,128)S(1)} %get-tuple-element.9), channel_id=1, replica_groups=mesh['phase'=2,'slab'=8,'arm'=2] {'slab'}, dimensions={0} | all-to-all | bytes 1048576 | tf_op jit(solution)/shard_map/all_to_all | solution.py:292
  23.3 4.6 %forward.1 = (f32[16,32,4,8,128]{4,3,2,1,0:T(8,128)S(1)}, f32[32,4,8,128]{3,2,1,0:T(8,128)S(1)}, f32[32,2,8,128]{3,2,1,0:T(8,128)S(1)}, f32[32,2,8,128]{3,2,1,0:T(8,128)S(1)}) custom-call(f32[9,8,128]{2,1,0:T(8,128)S(1)} %get-tuple-element.8.table_ref, f32[8,4,32,128]{3,2,1,0:T(8,128)S(1)} %all_to_all.20.field_ref), custom_call_target="tpu_custom_call" | custom-call | tf_op jit(solution)/shard_map/forward/pallas_call | solution.py:296
  27.9 0.1 collective-permute-start
  28.0 1.5 %collective-permute-done = f32[32,2,8,128]{3,2,1,0:T(8,128)S(1)} collective-permute-done((f32[32,2,8,128]{3,2,1,0:T(8,128)S(1)}, f32[32,2,8,128]{3,2,1,0:T(8,128)S(1)}, u32[]{:S(2)}, u32[]{:S(2)}) %collective-permute-start) | collective-permute-done | bytes 262176 | tf_op jit(solution)/shard_map/ppermute | solution.py:311
  29.5 15.0 %all_to_all.21.pairs_ref = f32[8,64,128]{2,1,0:T(8,128)S(1)} all-to-all(f32[8,64,128]{2,1,0:T(8,128)S(1)} %bitcast.3), channel_id=1, replica_groups=mesh['phase'=2,'slab'=8,'arm'=2] {'slab'}, dimensions={0} | all-to-all | bytes 524288 | tf_op jit(solution)/shard_map/all_to_all | solution.py:313
  44.5 0.1 exclusive.1
  44.6 12.0 %all_to_all.22 = f32[8,64,128]{2,1,0:T(8,128)S(1)} all-to-all(f32[8,64,128]{2,1,0:T(8,128)S(1)} %exclusive.1), channel_id=1, replica_groups=mesh['phase'=2,'slab'=8,'arm'=2] {'slab'}, dimensions={0} | all-to-all | bytes 524288 | tf_op jit(solution)/shard_map/all_to_all | solution.py:322
  56.5 0.1 fusion
  56.6 0.1 collective-permute-start.1
  56.7 1.5 %collective-permute-done.1.other_ref = f32[32,2,8,128]{3,2,1,0:T(8,128)S(1)} collective-permute-done((f32[32,2,8,128]{3,2,1,0:T(8,128)S(1)}, f32[32,2,8,128]{3,2,1,0:T(8,128)S(1)}, u32[]{:S(2)}, u32[]{:S(2)}) %collective-permute-start.1) | collective-permute-done | bytes 262176 | tf_op jit(solution)/shard_map/ppermute | solution.py:323
  58.2 7.9 %adjoint.1 = f32[16,72,128]{2,1,0:T(8,128)S(1)} custom-call(f32[9,8,128]{2,1,0:T(8,128)S(1)} %get-tuple-element.8.table_ref, f32[16,32,4,8,128]{4,3,2,1,0:T(8,128)S(1)} %get-tuple-element.10.hist_ref, f32[32,4,8,128]{3,2,1,0:T(8,128)S(1)} %get-tuple-element.11.half_ref, f32[32,2,8,128]{3,2,1,0:T(8,128)S(1)} %get-tuple-element.15.mine_ref, ...), custom_call_target="tpu_custom_call" | custom-call | tf_op jit(solution)/shard_map/adjoint/pallas_call | solution.py:326
  66.1 25.6 %all_to_all.23.shares_ref = f32[16,72,128]{2,1,0:T(8,128)S(1)} all-to-all(f32[16,72,128]{2,1,0:T(8,128)S(1)} %adjoint.1), channel_id=1, replica_groups=mesh['phase'=2,'slab'=8,'arm'=2] {'slab','arm'}, dimensions={0} | all-to-all | bytes 1179648 | tf_op jit(solution)/shard_map/all_to_all | solution.py:342
  91.7 0.7 owner.1
  (1 shorter events, 0.0 us)
Async XLA Ops:
  27.9 1.6 %collective-permute-start = (f32[32,2,8,128]{3,2,1,0:T(8,128)S(1)}, f32[32,2,8,128]{3,2,1,0:T(8,128)S(1)}, u32[]{:S(2)}, u32[]{:S(2)}) collective-permute-start(f32[32,2,8,128]{3,2,1,0:T(8,128)S(1)} %get-tuple-element.13), channel_id=1, source_target_pairs={{0,1},{1,0},{2,3},{3,2},{4,5},{5,4},{6,7},{7,6},{8,9},{9,8},{10,11... | collective-permute-start | bytes 786440 | tf_op jit(solution)/shard_map/ppermute | solution.py:311
  56.6 1.6 %collective-permute-start.1 = (f32[32,2,8,128]{3,2,1,0:T(8,128)S(1)}, f32[32,2,8,128]{3,2,1,0:T(8,128)S(1)}, u32[]{:S(2)}, u32[]{:S(2)}) collective-permute-start(f32[32,2,8,128]{3,2,1,0:T(8,128)S(1)} %get-tuple-element.14), channel_id=1, source_target_pairs={{0,1},{1,0},{2,3},{3,2},{4,5},{5,4},{6,7},{7,6},{8,9},{9,8},{10,11... | collective-permute-start | bytes 786440 | tf_op jit(solution)/shard_map/ppermute | solution.py:323

commit v4 on v3

--- a/solution.py
+++ b/solution.py
@@ -90,14 +90,14 @@
         slope_minus, slope = slope, slope_plus
 
 
-def in_pairs(count, step, first, second, carry):
-    def both(k, carry):
-        carry = step(2 * k, first, second, carry)
-        return lax.cond(
-            2 * k + 1 < count, lambda c: step(2 * k + 1, second, first, c), lambda c: c, carry
-        )
-
-    return lax.fori_loop(0, (count + 1) // 2, both, carry)
+def in_pairs(count, step, first, second):
+    lone = lax.rem(count, 2)
+    pl.when(lone == 1)(lambda: step(0, second, first))
+
+    @pl.loop(0, count // 2)
+    def _(pair):
+        step(lone + 2 * pair, first, second)
+        step(lone + 2 * pair + 1, second, first)
 
 
 def forward_kernel(table_ref, field_ref, hist_ref, half_ref, keep_ref, give_ref, gain_ref, *scratch):
@@ -108,16 +108,16 @@
     c_0 = 1.0 - 2.0 * (c_x + c_y + c_z)
     c_0, c_y, c_z, c_xy, c_xz, c_yz = (c / c_x for c in (c_0, c_y, c_z, c_xy, c_xz, c_yz))
     decay = -0.5 * mu
-    first, second = scratch[:3], scratch[3:]
+    start, first, second = (tuple(r.at[at] for r in scratch) for at in (lax.rem(count, 2), 0, 1))
 
     for x in range(planes):
         for j in range(parts):
             half = jnp.exp(decay * field_ref[x // depth, x % depth, pl.ds(j, ROWS, stride=parts), :])
             half_ref[x, j] = half
             gain_ref[x, j] = c_x * half
-            put(first, x, j, half)
-
-    def step(k, source, target, carry):
+            put(start, x, j, half)
+
+    def step(k, source, target):
         def visit(x, j, centre, sum_x, sum_y, sum_z, diff, slope_x, slope):
             if j == 0:
                 skew = [c_xy * d + c_yz * s for d, s in zip(diff, slope)]
@@ -130,9 +130,8 @@
             put(target, x, j, half_ref[x, j] * value)
 
         sweep(source, visit)
-        return carry
-
-    in_pairs(count, step, first, second, 0)
+
+    in_pairs(count, step, first, second)
     split = parts // 2
     for x in range(planes):
         for j in range(split):
@@ -160,12 +159,13 @@
 
 
 def adjoint_kernel(
-    table_ref, hist_ref, half_ref, mine_ref, other_ref, out_ref, square_ref, density_ref, line_ref, tail_ref, *scratch
+    table_ref, hist_ref, half_ref, mine_ref, other_ref, out_ref, square_ref, density_ref, line_ref, tail_ref,
+    total_ref, *scratch
 ):
     planes, parts, _, lanes = half_ref.shape
     core = lax.axis_index("arm")
     count, mu, (c_x, c_y, c_z, c_xy, c_xz, c_yz) = unpack(table_ref)
-    first, second = scratch[:3], scratch[3:]
+    start, first, second = (tuple(r.at[at] for r in scratch) for at in (lax.rem(count, 2), 0, 1))
     split = parts // 2
     zero = jnp.zeros((ROWS, lanes), jnp.float32)
 
@@ -178,13 +178,13 @@
                 half = half_ref[x, at]
                 value = half * adjoint
                 end = hist_ref[count - 1, x, at]
-                put(first, x, at, value)
+                put(start, x, at, value)
                 square_ref[x, at] = half * half
                 density_ref[x, at] = (-0.5 * end) * value
                 partition = partition + end * adjoint
 
-    def step(k, source, target, sums):
-        sums = list(sums)
+    def step(k, source, target):
+        sums = [total_ref[i] for i in range(6)]
 
         def visit(x, j, centre, sum_x, sum_y, sum_z, diff, slope_x, slope):
             if j == 0:
@@ -204,19 +204,18 @@
                 sums[i] = sums[i] + paired * term
 
         sweep(source, visit)
-        return tuple(sums)
-
-    sums = in_pairs(count, step, first, second, (zero,) * 6)
-
-    def finish(value_ref):
-        for x in range(planes):
-            for j in range(parts):
-                density = density_ref[x, j] + 0.5 * value_ref[x, j]
-                line_ref[x, pl.ds(j, ROWS, stride=parts), :] = mu * density / half_ref[x, j]
-
-    even = lax.rem(count, 2) == 0
-    pl.when(even)(lambda: finish(first[0]))
-    pl.when(jnp.logical_not(even))(lambda: finish(second[0]))
+        for i in range(6):
+            total_ref[i] = sums[i]
+
+    for i in range(6):
+        total_ref[i] = zero
+    in_pairs(count, step, first, second)
+    sums = [total_ref[i] for i in range(6)]
+
+    for x in range(planes):
+        for j in range(parts):
+            density = density_ref[x, j] + 0.5 * first[0][x, j]
+            line_ref[x, pl.ds(j, ROWS, stride=parts), :] = mu * density / half_ref[x, j]
 
     owners = out_ref.shape[0]
     cores = lax.axis_size("arm")
@@ -303,7 +302,7 @@
         ],
         in_specs=[vmem] * 2,
         out_specs=[vmem] * 4,
-        scratch_shapes=[pltpu.VMEM(grid, f32)] * 7,
+        scratch_shapes=[pltpu.VMEM(grid, f32)] + [pltpu.VMEM((2,) + grid, f32)] * 3,
         compiler_params=params,
         name="forward",
     )(table, field)
@@ -333,8 +332,9 @@
             pltpu.VMEM(grid, f32),
             pltpu.VMEM((planes, rows, lanes), f32),
             pltpu.VMEM((ROWS, lanes), f32),
+            pltpu.VMEM((6, ROWS, lanes), f32),
         ]
-        + [pltpu.VMEM(grid, f32)] * 6,
+        + [pltpu.VMEM((2,) + grid, f32)] * 3,
         compiler_params=params,
         name="adjoint",
     )(table, hist, half, rest * other, beyond)

time: 92.4 us -> 92.3 us (level)
  blocking collectives: 74.2 us -> 73 us
    all_to_all x1, blocking collectives: 15 us -> 14 us  [local(): lax.all_to_all((keep * other).reshape(flat), 'slab', 0, 0, tiled=True)]
where the time goes in v4:
time: 92.3 us; the launch traced here: 92 us
  blocking collectives  73 us (79%)
  Pallas kernels  14.5 us (16%)
  waiting for transfers between devices  2.68 us (3%)
  starting transfers between devices  1.06 us (1%)
    all_to_all x1, blocking collectives, local(): shares = lax.all_to_all(shares, ('slab', 'arm'), 0, 0, tiled=True)  24.9 us
    all_to_all x1, blocking collectives, local(): field = lax.all_to_all(chosen, 'slab', 0, 0, tiled=True)  21.6 us
    all_to_all x1, blocking collectives, local(): lax.all_to_all((keep * other).reshape(flat), 'slab', 0, 0, tiled=True)  14 us
    all_to_all x1, blocking collectives, local(): rest = lax.all_to_all(rest, 'slab', 0, 0, tiled=True).reshape(piece)  12.4 us
    pallas_call x1, Pallas kernels, local(): pl.pallas_call(adjoint_kernel, out_shape=jax.ShapeDtypeStruct((slabs * co...  7.99 us
    pallas_call x1, Pallas kernels, local(): pl.pallas_call(forward_kernel, out_shape=[jax.ShapeDtypeStruct((STEPS,) +...  4.73 us
  transfers between devices with their start and end apart: 2, of which 2 were waited for; matrix products, arithmetic and copies ran while one was open for 0% of the time, Pallas kernels for 0%

profile of v4, /device:TPU:0, one launch (start us, length us, event | category | flops | bytes accessed | tf_op | source)
XLA Modules:
  0.0 92.0 jit_solution(10850851605460897317)
XLA Ops:
  0.6 1.0 %prepare.1 = (f32[8,4,32,128]{3,2,1,0:T(8,128)S(1)}, f32[9,8,128]{2,1,0:T(8,128)S(1)}) custom-call(f32[8]{0:T(128)} %refs_0_.1, s32[8]{0:T(128)} %refs_1_.1, s32[8]{0:T(128)} %refs_2_.1, f32[6]{0:T(128)} %refs_3_.1, f32[2,4,32,128]{3,2,1,0:T(8,128)} %refs_4_.1), custom_call_target="tpu_custom_call" | custom-call | tf_op jit(solution)/shard_map/prepare/pallas_call | solution.py:278
  1.6 21.6 %all_to_all.20.field_ref = f32[8,4,32,128]{3,2,1,0:T(8,128)S(1)} all-to-all(f32[8,4,32,128]{3,2,1,0:T(8,128)S(1)} %get-tuple-element.9), channel_id=1, replica_groups=mesh['phase'=2,'slab'=8,'arm'=2] {'slab'}, dimensions={0} | all-to-all | bytes 1048576 | tf_op jit(solution)/shard_map/all_to_all | solution.py:291
  23.3 4.7 %forward.1 = (f32[16,32,4,8,128]{4,3,2,1,0:T(8,128)S(1)}, f32[32,4,8,128]{3,2,1,0:T(8,128)S(1)}, f32[32,2,8,128]{3,2,1,0:T(8,128)S(1)}, f32[32,2,8,128]{3,2,1,0:T(8,128)S(1)}) custom-call(f32[9,8,128]{2,1,0:T(8,128)S(1)} %get-tuple-element.8.table_ref, f32[8,4,32,128]{3,2,1,0:T(8,128)S(1)} %all_to_all.20.field_ref), custom_call_target="tpu_custom_call" | custom-call | tf_op jit(solution)/shard_map/forward/pallas_call | solution.py:295
  28.0 1.0 %collective-permute-start = (f32[32,2,8,128]{3,2,1,0:T(8,128)S(1)}, f32[32,2,8,128]{3,2,1,0:T(8,128)S(1)}, u32[]{:S(2)}, u32[]{:S(2)}) collective-permute-start(f32[32,2,8,128]{3,2,1,0:T(8,128)S(1)} %get-tuple-element.13), channel_id=1, source_target_pairs={{0,1},{1,0},{2,3},{3,2},{4,5},{5,4},{6,7},{7,6},{8,9},{9,8},{10,11... | collective-permute-start | bytes 786440 | tf_op jit(solution)/shard_map/ppermute | solution.py:310
  29.0 1.2 %collective-permute-done = f32[32,2,8,128]{3,2,1,0:T(8,128)S(1)} collective-permute-done((f32[32,2,8,128]{3,2,1,0:T(8,128)S(1)}, f32[32,2,8,128]{3,2,1,0:T(8,128)S(1)}, u32[]{:S(2)}, u32[]{:S(2)}) %collective-permute-start) | collective-permute-done | bytes 262176 | tf_op jit(solution)/shard_map/ppermute | solution.py:310
  30.2 14.0 %all_to_all.21.pairs_ref = f32[8,64,128]{2,1,0:T(8,128)S(1)} all-to-all(f32[8,64,128]{2,1,0:T(8,128)S(1)} %bitcast.3), channel_id=1, replica_groups=mesh['phase'=2,'slab'=8,'arm'=2] {'slab'}, dimensions={0} | all-to-all | bytes 524288 | tf_op jit(solution)/shard_map/all_to_all | solution.py:312
  44.2 0.1 exclusive.1
  44.3 12.4 %all_to_all.22 = f32[8,64,128]{2,1,0:T(8,128)S(1)} all-to-all(f32[8,64,128]{2,1,0:T(8,128)S(1)} %exclusive.1), channel_id=1, replica_groups=mesh['phase'=2,'slab'=8,'arm'=2] {'slab'}, dimensions={0} | all-to-all | bytes 524288 | tf_op jit(solution)/shard_map/all_to_all | solution.py:321
  56.7 0.1 fusion
  56.8 0.1 collective-permute-start.1
  56.8 1.5 %collective-permute-done.1.other_ref = f32[32,2,8,128]{3,2,1,0:T(8,128)S(1)} collective-permute-done((f32[32,2,8,128]{3,2,1,0:T(8,128)S(1)}, f32[32,2,8,128]{3,2,1,0:T(8,128)S(1)}, u32[]{:S(2)}, u32[]{:S(2)}) %collective-permute-start.1) | collective-permute-done | bytes 262176 | tf_op jit(solution)/shard_map/ppermute | solution.py:322
  58.4 8.0 %adjoint.1 = f32[16,72,128]{2,1,0:T(8,128)S(1)} custom-call(f32[9,8,128]{2,1,0:T(8,128)S(1)} %get-tuple-element.8.table_ref, f32[16,32,4,8,128]{4,3,2,1,0:T(8,128)S(1)} %get-tuple-element.10.hist_ref, f32[32,4,8,128]{3,2,1,0:T(8,128)S(1)} %get-tuple-element.11.half_ref, f32[32,2,8,128]{3,2,1,0:T(8,128)S(1)} %get-tuple-element.15.mine_ref, ...), custom_call_target="tpu_custom_call" | custom-call | tf_op jit(solution)/shard_map/adjoint/pallas_call | solution.py:325
  66.4 24.9 %all_to_all.23.shares_ref = f32[16,72,128]{2,1,0:T(8,128)S(1)} all-to-all(f32[16,72,128]{2,1,0:T(8,128)S(1)} %adjoint.1), channel_id=1, replica_groups=mesh['phase'=2,'slab'=8,'arm'=2] {'slab','arm'}, dimensions={0} | all-to-all | bytes 1179648 | tf_op jit(solution)/shard_map/all_to_all | solution.py:342
  91.3 0.7 owner.1
  (1 shorter events, 0.0 us)
Async XLA Ops:
  28.0 2.1 %collective-permute-start = (f32[32,2,8,128]{3,2,1,0:T(8,128)S(1)}, f32[32,2,8,128]{3,2,1,0:T(8,128)S(1)}, u32[]{:S(2)}, u32[]{:S(2)}) collective-permute-start(f32[32,2,8,128]{3,2,1,0:T(8,128)S(1)} %get-tuple-element.13), channel_id=1, source_target_pairs={{0,1},{1,0},{2,3},{3,2},{4,5},{5,4},{6,7},{7,6},{8,9},{9,8},{10,11... | collective-permute-start | bytes 786440 | tf_op jit(solution)/shard_map/ppermute | solution.py:310
  56.8 1.6 %collective-permute-start.1 = (f32[32,2,8,128]{3,2,1,0:T(8,128)S(1)}, f32[32,2,8,128]{3,2,1,0:T(8,128)S(1)}, u32[]{:S(2)}, u32[]{:S(2)}) collective-permute-start(f32[32,2,8,128]{3,2,1,0:T(8,128)S(1)} %get-tuple-element.14), channel_id=1, source_target_pairs={{0,1},{1,0},{2,3},{3,2},{4,5},{5,4},{6,7},{7,6},{8,9},{9,8},{10,11... | collective-permute-start | bytes 786440 | tf_op jit(solution)/shard_map/ppermute | solution.py:322
